TPU v7x, 32 devices: a whole 2x2x4 slice. The times are simulated.
32 devices in a mesh: dp: 8 (over z, x), tensor: 4 (over y, core).
Axes of the slice: x: 2, y: 2, z: 4, core: 2. Of those that a mesh axis runs over, the one named last changes fastest.
Arguments:
- patches: bfloat16 [16384, 768], P(('dp', 'tensor')), may hold values from -6 to 6
- counts: int32 [8, 3], P('dp'), may hold values from 1 to 2, as said below
- norm_gain: float32 [2, 768], replicated, may hold values from 0.5 to 1.5
- norm_bias: float32 [2, 768], replicated, may hold values from -3 to 3
- w_qkv: bfloat16 [768, 3, 768], P(None, None, 'tensor'), may hold values from -0.21875 to 0.21875
- b_qv: float32 [2, 768], P(None, 'tensor'), may hold values from -3 to 3
- w_out: bfloat16 [768, 768], P('tensor'), may hold values from -0.625 to 0.625
- out_bias: float32 [2, 768], replicated, may hold values from -3 to 3
- w_up: bfloat16 [768, 3072], P(None, 'tensor'), may hold values from -0.21875 to 0.21875
- b_up: float32 [3072], P('tensor'), may hold values from -3 to 3
- w_down: bfloat16 [3072, 768], P('tensor'), may hold values from -0.109375 to 0.109375
- cotangent: bfloat16 [16384, 768], P(('dp', 'tensor')), may hold values from -6 to 6
Outputs:
- encoded: bfloat16 [16384, 768], P(('dp', 'tensor'))
- patches_grad: bfloat16 [16384, 768], P(('dp', 'tensor'))
- norm_gain_grad: float32 [2, 768], replicated
- norm_bias_grad: float32 [2, 768], replicated
- w_qkv_grad: float32 [768, 3, 768], P('dp', None, 'tensor')
- b_qv_grad: float32 [2, 768], replicated
- w_out_grad: float32 [768, 768], P('tensor', 'dp')
- out_bias_grad: float32 [2, 768], replicated
- w_up_grad: float32 [768, 3072], P('dp', 'tensor')
- b_up_grad: float32 [3072], replicated
- w_down_grad: float32 [3072, 768], P('tensor', 'dp')
Inputs may be any that keep to these rules, and one draw needn't show every extreme that they name: `counts`: in every column some group has exactly 2 images of that size; every group has at least one image of each size.
All inputs are finite; a program needn't handle non-finite values.
Results may differ from a plain program's by a relative error of at most 0.015.
Values may be sent and summed in bfloat16 or wider, within the bound.
A program may use at most 192 MiB of HBM per device.

v0:
```python
import jax
import jax.numpy as jnp
from jax import lax
from jax.sharding import PartitionSpec as P

D = 768
HEADS = 12
HEAD_DIM = 64
FF = 3072
SIDE_S = 12
SIDE_M = 15
SIDE_L = 20
BLOCK = 512
TOK_DEV = 2048


EPSILON = 1e-06


def layout(group_counts):
    positions = jnp.arange(TOK_DEV, dtype=jnp.int32)
    area_small = SIDE_S * SIDE_S
    area_middle = SIDE_M * SIDE_M
    area_large = SIDE_L * SIDE_L
    end_small = group_counts[0] * area_small
    end_middle = end_small + group_counts[1] * area_middle
    end_large = end_middle + group_counts[2] * area_large
    size_class = (positions >= end_small).astype(jnp.int32) + (positions >= end_middle).astype(
        jnp.int32
    )
    begins = jnp.where(size_class == 0, 0, jnp.where(size_class == 1, end_small, end_middle))
    area_len = jnp.where(
        size_class == 0, area_small, jnp.where(size_class == 1, area_middle, area_large)
    )
    side_len = jnp.where(size_class == 0, SIDE_S, jnp.where(size_class == 1, SIDE_M, SIDE_L))
    within = positions - begins
    picture_index = within // area_len
    within_image = within % area_len
    is_valid = positions < end_large
    segment = jnp.where(is_valid, size_class * 16 + picture_index, 255)
    grid_row = (within_image // side_len).astype(jnp.float32)
    grid_col = (within_image % side_len).astype(jnp.float32)
    return (segment, grid_row, grid_col, is_valid.astype(jnp.float32))


def normalize(values, gain_row, shift_row):
    centred = values - jnp.mean(values, axis=-1, keepdims=True)
    spread = jnp.mean(centred * centred, axis=-1, keepdims=True)
    return centred * lax.rsqrt(spread + EPSILON) * gain_row + shift_row


def slopes_of(first_head, count_heads):
    head_number = (first_head + jnp.arange(count_heads, dtype=jnp.int32)).astype(jnp.float32) + 1.0
    return jnp.exp2(-8.0 * head_number / HEADS)


def distances(row_query, col_query, row_key, col_key):
    delta_row = row_query[:, None] - row_key[None, :]
    delta_col = col_query[:, None] - col_key[None, :]
    return jnp.sqrt(delta_row * delta_row + delta_col * delta_col)


def on_device(
    patches,
    counts,
    norm_gain,
    norm_bias,
    w_qkv,
    b_qv,
    w_out,
    out_bias,
    w_up,
    b_up,
    w_down,
    cotangent,
):
    local_rows = patches.shape[0]
    width_here = w_qkv.shape[2]
    heads_here = width_here // HEAD_DIM
    ff_here = w_up.shape[1]
    tensor_pos = lax.axis_index("tensor")
    score_scale = HEAD_DIM ** (-0.5)
    block_count = TOK_DEV // BLOCK
    segment, grid_row, grid_col, is_valid = layout(counts[0])
    keep_rows = lax.dynamic_slice_in_dim(is_valid, tensor_pos * local_rows, local_rows)[:, None]
    slopes = slopes_of(tensor_pos * heads_here, heads_here)
    inputs = patches.astype(jnp.float32)
    normed_local = normalize(inputs, norm_gain[0], norm_bias[0]).astype(jnp.bfloat16)
    normed = lax.all_gather(normed_local, "tensor", axis=0, tiled=True)
    projected = jnp.einsum("td,dsc->tsc", normed, w_qkv, preferred_element_type=jnp.float32)
    queries = (projected[:, 0] + b_qv[0]).astype(jnp.bfloat16)
    key_heads = projected[:, 1].astype(jnp.bfloat16).reshape(TOK_DEV, heads_here, HEAD_DIM)
    value_heads = (
        (projected[:, 2] + b_qv[1]).astype(jnp.bfloat16).reshape(TOK_DEV, heads_here, HEAD_DIM)
    )

    def block_scores(offset):
        query_block = lax.dynamic_slice_in_dim(queries, offset, BLOCK).reshape(
            BLOCK, heads_here, HEAD_DIM
        )
        raw_scores = (
            jnp.einsum("qhe,khe->hqk", query_block, key_heads, preferred_element_type=jnp.float32)
            * score_scale
        )
        near_dist = distances(
            lax.dynamic_slice_in_dim(grid_row, offset, BLOCK),
            lax.dynamic_slice_in_dim(grid_col, offset, BLOCK),
            grid_row,
            grid_col,
        )
        same_image = lax.dynamic_slice_in_dim(segment, offset, BLOCK)[:, None] == segment[None, :]
        return (
            query_block,
            jnp.where(
                same_image[None], raw_scores - slopes[:, None, None] * near_dist[None], -1e30
            ),
        )

    def attend_block(block_index):
        _, scores = block_scores(block_index * BLOCK)
        highest_score = jnp.max(scores, axis=-1, keepdims=True)
        exp_terms = jnp.exp(scores - highest_score)
        totals = jnp.sum(exp_terms, axis=-1, keepdims=True)
        weights = (exp_terms / totals).astype(jnp.bfloat16)
        mixed_block = jnp.einsum(
            "hqk,khe->qhe", weights, value_heads, preferred_element_type=jnp.float32
        )
        return (
            mixed_block.reshape(BLOCK, width_here).astype(jnp.bfloat16),
            highest_score[..., 0] + jnp.log(totals[..., 0]),
        )

    mixed_blocks, log_totals = lax.map(attend_block, jnp.arange(block_count, dtype=jnp.int32))
    mixed_rows = mixed_blocks.reshape(TOK_DEV, width_here)
    attended = lax.psum_scatter(
        jnp.dot(mixed_rows, w_out, preferred_element_type=jnp.float32).astype(jnp.bfloat16),
        "tensor",
        scatter_dimension=0,
        tiled=True,
    ).astype(jnp.float32)
    after_attn = inputs + keep_rows * (attended + out_bias[0])
    normed_two_local = normalize(after_attn, norm_gain[1], norm_bias[1]).astype(jnp.bfloat16)
    normed_two = lax.all_gather(normed_two_local, "tensor", axis=0, tiled=True)
    hidden_pre = jnp.dot(normed_two, w_up, preferred_element_type=jnp.float32) + b_up
    hidden = jax.nn.gelu(hidden_pre, approximate=False).astype(jnp.bfloat16)
    branch = lax.psum_scatter(
        jnp.dot(hidden, w_down, preferred_element_type=jnp.float32).astype(jnp.bfloat16),
        "tensor",
        scatter_dimension=0,
        tiled=True,
    ).astype(jnp.float32)
    result = (after_attn + keep_rows * (branch + out_bias[1])).astype(jnp.bfloat16)
    upstream = cotangent.astype(jnp.float32)
    down_bias_grad = jnp.sum(keep_rows * upstream, axis=0)
    branch_grad = lax.all_gather(
        (keep_rows * upstream).astype(jnp.bfloat16), "tensor", axis=0, tiled=True
    )
    w_down_grad = jnp.einsum("tf,td->fd", hidden, branch_grad, preferred_element_type=jnp.float32)
    hidden_grad = jnp.einsum("td,fd->tf", branch_grad, w_down, preferred_element_type=jnp.float32)
    _, gelu_back = jax.vjp(lambda pre_act: jax.nn.gelu(pre_act, approximate=False), hidden_pre)
    pre_grad = gelu_back(hidden_grad)[0].astype(jnp.bfloat16)
    up_bias_grad = jnp.sum(pre_grad, axis=0, dtype=jnp.float32)
    w_up_grad = jnp.einsum("td,tf->df", normed_two, pre_grad, preferred_element_type=jnp.float32)
    normed_two_grad = lax.psum_scatter(
        jnp.einsum("tf,df->td", pre_grad, w_up, preferred_element_type=jnp.float32).astype(
            jnp.bfloat16
        ),
        "tensor",
        scatter_dimension=0,
        tiled=True,
    ).astype(jnp.float32)
    _, norm_two_back = jax.vjp(normalize, after_attn, norm_gain[1], norm_bias[1])
    through_two, gain_two_grad, shift_two_grad = norm_two_back(normed_two_grad)
    after_grad = upstream + through_two
    attn_bias_grad = jnp.sum(keep_rows * after_grad, axis=0)
    attn_local = (keep_rows * after_grad).astype(jnp.bfloat16)
    attn_grad = lax.all_gather(attn_local, "tensor", axis=0, tiled=True)
    w_out_grad = jnp.einsum("tc,td->cd", mixed_rows, attn_grad, preferred_element_type=jnp.float32)
    mixed_grad = jnp.einsum(
        "td,cd->tc", attn_grad, w_out, preferred_element_type=jnp.float32
    ).astype(jnp.bfloat16)
    mixed_heads = mixed_grad.reshape(TOK_DEV, heads_here, HEAD_DIM)

    def back_block(running, block_index):
        key_acc, value_acc = running
        offset = block_index * BLOCK
        query_block, scores = block_scores(offset)
        weights = jnp.exp(
            scores - lax.dynamic_index_in_dim(log_totals, block_index, keepdims=False)[..., None]
        )
        grad_block = lax.dynamic_slice_in_dim(mixed_heads, offset, BLOCK)
        value_acc = value_acc + jnp.einsum(
            "hqk,qhe->khe",
            weights.astype(jnp.bfloat16),
            grad_block,
            preferred_element_type=jnp.float32,
        )
        weight_grad = jnp.einsum(
            "qhe,khe->hqk", grad_block, value_heads, preferred_element_type=jnp.float32
        )
        score_grad = (
            weights * (weight_grad - jnp.sum(weights * weight_grad, axis=-1, keepdims=True))
        ).astype(jnp.bfloat16)
        query_grad_block = (
            jnp.einsum("hqk,khe->qhe", score_grad, key_heads, preferred_element_type=jnp.float32)
            * score_scale
        )
        key_acc = (
            key_acc
            + jnp.einsum(
                "hqk,qhe->khe", score_grad, query_block, preferred_element_type=jnp.float32
            )
            * score_scale
        )
        return (
            (key_acc, value_acc),
            query_grad_block.reshape(BLOCK, width_here).astype(jnp.bfloat16),
        )

    zero_heads = jnp.zeros((TOK_DEV, heads_here, HEAD_DIM), jnp.float32)
    (key_acc, value_acc), query_blocks = lax.scan(
        back_block, (zero_heads, zero_heads), jnp.arange(block_count, dtype=jnp.int32)
    )
    query_grad = query_blocks.reshape(TOK_DEV, width_here)
    key_grad = key_acc.reshape(TOK_DEV, width_here).astype(jnp.bfloat16)
    value_grad = value_acc.reshape(TOK_DEV, width_here).astype(jnp.bfloat16)
    projected_grad = jnp.stack([query_grad, key_grad, value_grad], axis=1)
    qv_bias_grad = jnp.stack(
        [
            jnp.sum(query_grad, axis=0, dtype=jnp.float32),
            jnp.sum(value_grad, axis=0, dtype=jnp.float32),
        ]
    )
    w_qkv_grad = jnp.einsum(
        "td,tsc->dsc", normed, projected_grad, preferred_element_type=jnp.float32
    )
    normed_grad = lax.psum_scatter(
        jnp.einsum("tsc,dsc->td", projected_grad, w_qkv, preferred_element_type=jnp.float32).astype(
            jnp.bfloat16
        ),
        "tensor",
        scatter_dimension=0,
        tiled=True,
    ).astype(jnp.float32)
    qv_full = lax.dynamic_update_slice_in_dim(
        jnp.zeros((2, D), jnp.float32), qv_bias_grad, tensor_pos * width_here, 1
    )
    _, norm_one_back = jax.vjp(normalize, inputs, norm_gain[0], norm_bias[0])
    through_one, gain_one_grad, shift_one_grad = norm_one_back(normed_grad)
    input_grad = (after_grad + through_one).astype(jnp.bfloat16)
    up_full = lax.dynamic_update_slice_in_dim(
        jnp.zeros((FF,), jnp.float32), up_bias_grad, tensor_pos * ff_here, 0
    )
    gains_grad, shifts_grad, outer_grad, qv_sum, up_sum = lax.psum(
        (
            jnp.stack([gain_one_grad, gain_two_grad]),
            jnp.stack([shift_one_grad, shift_two_grad]),
            jnp.stack([attn_bias_grad, down_bias_grad]),
            qv_full,
            up_full,
        ),
        ("dp", "tensor"),
    )
    qkv_part, out_part, up_part, down_part = (
        lax.psum_scatter(w_qkv_grad, "dp", scatter_dimension=0, tiled=True),
        lax.psum_scatter(w_out_grad, "dp", scatter_dimension=1, tiled=True),
        lax.psum_scatter(w_up_grad, "dp", scatter_dimension=0, tiled=True),
        lax.psum_scatter(w_down_grad, "dp", scatter_dimension=1, tiled=True),
    )
    return (
        result,
        input_grad,
        gains_grad,
        shifts_grad,
        qkv_part,
        qv_sum,
        out_part,
        outer_grad,
        up_part,
        up_sum,
        down_part,
    )


def solution(mesh):
    placed = (
        P(("dp", "tensor"), None),
        P("dp", None),
        P(),
        P(),
        P(None, None, "tensor"),
        P(None, "tensor"),
        P("tensor", None),
        P(),
        P(None, "tensor"),
        P("tensor"),
        P("tensor", None),
        P(("dp", "tensor"), None),
    )
    return jax.shard_map(
        on_device,
        mesh=mesh,
        in_specs=placed,
        out_specs=(
            P(("dp", "tensor"), None),
            P(("dp", "tensor"), None),
            P(),
            P(),
            P("dp", None, "tensor"),
            P(),
            P("tensor", "dp"),
            P(),
            P("dp", "tensor"),
            P(),
            P("tensor", "dp"),
        ),
        check_vma=False,
    )
```

profile of v0, /device:TPU:0, one launch (start us, length us, event | category | flops | bytes accessed | tf_op | source)
XLA Modules:
  0.0 811.1 jit_solution(15307755754679857029)
XLA Ops:
  19.1 26.9 %all-gather.5.cloned.1.call-done = bf16[2048,768]{1,0:T(8,128)(2,1)} async-done(((bf16[512,768]{1,0:T(8,128)(2,1)}), bf16[2048,768]{1,0:T(8,128)(2,1)}) %all-gather.5.cloned.1.call-update) | async-done | bytes 3145744 | tf_op jit(solution)/shard_map/all_gather | solution.py:89
  52.4 80.2 %while.28 = (s32[]{:T(128)}, bf16[4,512,192]{1,2,0:T(8,128)(2,1)}, f32[4,3,512]{2,1,0:T(4,128)}, s32[4]{0:T(128)}, s32[2048]{0:T(1024)S(1)}, /*index=5*/bf16[204...) while((s32[]{:T(128)}, bf16[4,512,192]{1,2,0:T(8,128)(2,1)}, ...), condition=%wide.region_5.6_spmd.clone, body=%wide.region_2.5_spmd.clone.sunk | while | flops 868317696 | bytes 61567260 | solution.py:133
  140.7 36.2 %reduce-scatter.11.cloned.1.call-done = bf16[512,768]{1,0:T(8,128)(2,1)} async-done(((bf16[2048,768]{1,0:T(8,128)(2,1)}), bf16[512,768]{1,0:T(8,128)(2,1)}) %reduce-scatter.11.cloned.1.call-update) | async-done | bytes 786448 | tf_op jit(solution)/shard_map/reduce_scatter | solution.py:135
  184.6 28.0 %all-gather.7.cloned.1.call-done = bf16[2048,768]{1,0:T(8,128)(2,1)} async-done(((bf16[512,768]{1,0:T(8,128)(2,1)}), bf16[2048,768]{1,0:T(8,128)(2,1)}) %all-gather.7.cloned.1.call-update) | async-done | bytes 3145744 | tf_op jit(solution)/shard_map/all_gather | solution.py:143
  212.6 7.5 fusion.74
  220.1 23.0 %all-gather.9.cloned.1.call-done = bf16[2048,768]{1,0:T(8,128)(2,1)} async-done(((bf16[512,768]{1,0:T(8,128)(2,1)}), bf16[2048,768]{1,0:T(8,128)(2,1)}) %all-gather.9.cloned.1.call-update) | async-done | bytes 3145744 | tf_op jit(solution)/shard_map/all_gather | solution.py:155
  243.2 20.2 %convert_reduce_fusion = (f32[768]{0:T(1024)}, bf16[2048,768]{1,0:T(8,128)(2,1)S(1)}, f32[2048,768]{1,0:T(8,128)}) fusion(f32[2048,768]{1,0:T(8,128)} %fusion.74, f32[768]{0:T(1024)} %param.25, bf16[2048,768]{1,0:T(8,128)(2,1)} %all-gather.9.cloned.1.call-done, bf16[768,768]{1,0:T(8,128)(2,1)S(1)} %copy-done), kind=kOutput, calls=%fused_computation.43 | convolution fusion | flops 2533883136 | bytes 20060160 | tf_op jit(solution)/shard_map/td,fd->tf/dot_general | solution.py:159
  280.6 26.5 %reduce-scatter.15.cloned.1.call-done = bf16[512,768]{1,0:T(8,128)(2,1)} async-done(((bf16[2048,768]{1,0:T(8,128)(2,1)}), bf16[512,768]{1,0:T(8,128)(2,1)}) %reduce-scatter.15.cloned.1.call-update) | async-done | bytes 786448 | tf_op jit(solution)/shard_map/reduce_scatter | solution.py:164
  309.8 37.6 %reduce-scatter.13.cloned.1.call-done = bf16[512,768]{1,0:T(8,128)(2,1)} async-done(((bf16[2048,768]{1,0:T(8,128)(2,1)}), bf16[512,768]{1,0:T(8,128)(2,1)}) %reduce-scatter.13.cloned.1.call-update) | async-done | bytes 786448 | tf_op jit(solution)/shard_map/reduce_scatter | solution.py:146
  354.0 28.6 %all-gather.11.cloned.1.call-done = bf16[2048,768]{1,0:T(8,128)(2,1)} async-done(((bf16[512,768]{1,0:T(8,128)(2,1)}), bf16[2048,768]{1,0:T(8,128)(2,1)}) %all-gather.11.cloned.1.call-update) | async-done | bytes 3145744 | tf_op jit(solution)/shard_map/all_gather | solution.py:177
  391.7 141.8 %while.29 = (s32[]{:T(128)}, f32[2048,3,64]{0,2,1:T(8,128)}, f32[2048,3,64]{0,2,1:T(8,128)}, bf16[4,512,192]{1,2,0:T(8,128)(2,1)}, s32[4]{0:T(128)S(1)}, /*index...) while((s32[]{:T(128)}, f32[2048,3,64]{0,2,1:T(8,128)}, ...), condition=%wide.region_15.16_spmd.clone, body=%wide.region_13.15_spmd.clone.sunk | while | flops 2056321536 | bytes 143663600 | solution.py:221
  401.9 8.7 %multiply_reduce_fusion.4 = (f32[3,512]{1,0:T(4,128)S(1)}, f32[3,512,2048]{2,1,0:T(8,128)}) fusion(f32[3,512,2048]{2,1,0:T(8,128)S(1)} %fusion.144, f32[3,512]{1,0:T(4,128)S(1)} %dynamic-slice_bitcast_fusion.2, f32[512,2048]{1,0:T(8,128)S(1)} %add_sqrt_fusion.5, f32[3]{0:T(128)S(1)} %multiply_exponential_fusion.5, ...), kind=kOutput, calls=%fused_computation.18.clone.1 | convolution fusion | flops 424671744 | bytes 31404044 | tf_op jit(solution)/shard_map/while/body/eval_jaxpr/qhe,khe->hqk/dot_general | solution.py:102
  410.6 5.6 multiply_convert_fusion.4
  416.3 6.2 fusion.146
  437.4 8.7 %multiply_reduce_fusion.4 = (f32[3,512]{1,0:T(4,128)S(1)}, f32[3,512,2048]{2,1,0:T(8,128)}) fusion(f32[3,512,2048]{2,1,0:T(8,128)S(1)} %fusion.144, f32[3,512]{1,0:T(4,128)S(1)} %dynamic-slice_bitcast_fusion.2, f32[512,2048]{1,0:T(8,128)S(1)} %add_sqrt_fusion.5, f32[3]{0:T(128)S(1)} %multiply_exponential_fusion.5, ...), kind=kOutput, calls=%fused_computation.18.clone.1 | convolution fusion | flops 424671744 | bytes 31404044 | tf_op jit(solution)/shard_map/while/body/eval_jaxpr/qhe,khe->hqk/dot_general | solution.py:102
  446.1 5.6 multiply_convert_fusion.4
  451.7 6.1 fusion.146
  472.8 8.7 %multiply_reduce_fusion.4 = (f32[3,512]{1,0:T(4,128)S(1)}, f32[3,512,2048]{2,1,0:T(8,128)}) fusion(f32[3,512,2048]{2,1,0:T(8,128)S(1)} %fusion.144, f32[3,512]{1,0:T(4,128)S(1)} %dynamic-slice_bitcast_fusion.2, f32[512,2048]{1,0:T(8,128)S(1)} %add_sqrt_fusion.5, f32[3]{0:T(128)S(1)} %multiply_exponential_fusion.5, ...), kind=kOutput, calls=%fused_computation.18.clone.1 | convolution fusion | flops 424671744 | bytes 31404044 | tf_op jit(solution)/shard_map/while/body/eval_jaxpr/qhe,khe->hqk/dot_general | solution.py:102
  481.5 5.6 multiply_convert_fusion.4
  487.1 6.1 fusion.146
  508.2 8.7 %multiply_reduce_fusion.4 = (f32[3,512]{1,0:T(4,128)S(1)}, f32[3,512,2048]{2,1,0:T(8,128)}) fusion(f32[3,512,2048]{2,1,0:T(8,128)S(1)} %fusion.144, f32[3,512]{1,0:T(4,128)S(1)} %dynamic-slice_bitcast_fusion.2, f32[512,2048]{1,0:T(8,128)S(1)} %add_sqrt_fusion.5, f32[3]{0:T(128)S(1)} %multiply_exponential_fusion.5, ...), kind=kOutput, calls=%fused_computation.18.clone.1 | convolution fusion | flops 424671744 | bytes 31404044 | tf_op jit(solution)/shard_map/while/body/eval_jaxpr/qhe,khe->hqk/dot_general | solution.py:102
  516.9 5.6 multiply_convert_fusion.4
  522.5 6.1 fusion.146
  540.0 5.7 bitcast_convert_fusion
  545.8 7.0 fusion.76
  552.9 7.8 fusion.75
  561.0 6.0 fusion.32
  576.5 7.3 reduce-scatter.17.cloned.1.call-done
  590.2 41.6 %all-reduce = (f32[2,768]{1,0:T(2,128)}, f32[2,768]{1,0:T(2,128)}, f32[2,768]{1,0:T(2,128)}, f32[2,768]{1,0:T(2,128)}, f32[3072]{0:T(1024)}) all-reduce(f32[2,768]{1,0:T(2,128)} %pad_maximum_fusion.3, f32[2,768]{1,0:T(2,128)} %pad_maximum_fusion.4, ...), channel_id=1, replica_groups=mesh['dp'=8,'tensor'=4] {'dp','tensor'}, use_global_device_ids=true, to_apply=%region_21.22 | all-reduce | flops 9216 | bytes 73728 | tf_op jit(solution)/shard_map/psum | solution.py:254
  635.5 22.4 %reduce-scatter.23.cloned.1.call-done = f32[768,96]{0,1:T(8,128)} async-done(((f32[768,768]{0,1:T(8,128)}), f32[768,96]{0,1:T(8,128)}) %reduce-scatter.23.cloned.1.call-update) | async-done | bytes 294928 | tf_op jit(solution)/shard_map/reduce_scatter | solution.py:268
  658.0 72.9 %reduce-scatter.21.cloned.1.call-done = f32[96,768]{1,0:T(8,128)} async-done(((f32[768,768]{1,0:T(8,128)}), f32[96,768]{1,0:T(8,128)}) %reduce-scatter.21.cloned.1.call-update) | async-done | bytes 294928 | tf_op jit(solution)/shard_map/reduce_scatter | solution.py:267
  730.9 72.9 %reduce-scatter.19.cloned.1.call-done = f32[96,3,192]{2,0,1:T(8,128)} async-done(((f32[768,3,192]{2,0,1:T(8,128)}), f32[96,3,192]{2,0,1:T(8,128)}) %reduce-scatter.19.cloned.1.call-update) | async-done | bytes 221200 | tf_op jit(solution)/shard_map/reduce_scatter | solution.py:265
  (340 shorter events, 220.0 us)
Async XLA Ops:
  7.2 236.0 %copy-start = (bf16[768,768]{1,0:T(8,128)(2,1)S(1)}, bf16[768,768]{1,0:T(8,128)(2,1)}, u32[]{:S(2)}) copy-start(bf16[768,768]{1,0:T(8,128)(2,1)} %param.26) | copy-start | bytes 3538948
  7.2 38.8 %copy-start.54 = (bf16[768,3,192]{0,2,1:T(8,128)(2,1)S(1)}, bf16[768,3,192]{0,2,1:T(8,128)(2,1)}, u32[]{:S(2)}) copy-start(bf16[768,3,192]{0,2,1:T(8,128)(2,1)} %param.20) | copy-start | bytes 2654212
  7.2 38.8 %all-gather.5.cloned.1.call-start = ((), (), s32[]{:S(2)}) async-start(), calls=%async_computation.8 | async-start | bytes 3932160 | tf_op jit(solution)/shard_map/all_gather | solution.py:89
  8.7 41.2 %copy-start.31 = (f32[512]{0:T(512)}, f32[512]{0:T(512)S(1)}, u32[]{:S(2)}) copy-start(f32[512]{0:T(512)S(1)} %broadcast_multiply_fusion.1) | copy-start | bytes 6148
  10.8 39.1 %copy-start.37 = (f32[512]{0:T(512)}, f32[512]{0:T(512)S(1)}, u32[]{:S(2)}) copy-start(f32[512]{0:T(512)S(1)} %fusion.65) | copy-start | bytes 6148
  12.2 37.7 %copy-start.27 = (f32[768]{0:T(1024)}, f32[768]{0:T(1024)S(1)}, u32[]{:S(2)}) copy-start(f32[768]{0:T(1024)S(1)} %get-tuple-element.314) | copy-start | bytes 9220
  14.6 162.3 %reduce-scatter.11.cloned.1.call-start = ((), (), s32[]{:S(2)}) async-start(), calls=%async_computation.9 | async-start | bytes 3932160 | tf_op jit(solution)/shard_map/reduce_scatter | solution.py:135
  138.9 38.1 %copy-start.2 = (bf16[512,768]{1,0:T(8,128)(2,1)S(1)}, bf16[512,768]{1,0:T(8,128)(2,1)}, u32[]{:S(2)}) copy-start(bf16[512,768]{1,0:T(8,128)(2,1)} %param.16) | copy-start | bytes 2359300
  138.9 73.7 %all-gather.7.cloned.1.call-start = ((), (), s32[]{:S(2)}) async-start(), calls=%async_computation.10 | async-start | bytes 3932160 | tf_op jit(solution)/shard_map/all_gather | solution.py:143
  184.0 59.2 %all-gather.9.cloned.1.call-start = ((), (), s32[]{:S(2)}) async-start(), calls=%async_computation.12 | async-start | bytes 3932160 | tf_op jit(solution)/shard_map/all_gather | solution.py:155
  184.5 122.5 %reduce-scatter.15.cloned.1.call-start = ((), (), s32[]{:S(2)}) async-start(), calls=%async_computation.13 | async-start | bytes 3932160 | tf_op jit(solution)/shard_map/reduce_scatter | solution.py:164
  243.2 21.8 %copy-start.53 = (bf16[768,768]{1,0:T(8,128)(2,1)S(1)}, bf16[768,768]{1,0:T(8,128)(2,1)}, u32[]{:S(2)}) copy-start(bf16[768,768]{1,0:T(8,128)(2,1)} %param.24) | copy-start | bytes 3538948
  269.0 78.3 %reduce-scatter.13.cloned.1.call-start = ((), (), s32[]{:S(2)}) async-start(), calls=%async_computation.11 | async-start | bytes 3932160 | tf_op jit(solution)/shard_map/reduce_scatter | solution.py:146
  280.3 26.8 %copy-start.26 = (f32[768]{0:T(1024)S(1)}, f32[768]{0:T(1024)}, u32[]{:S(2)}) copy-start(f32[768]{0:T(1024)} %get-tuple-element.231) | copy-start | bytes 9220
  280.3 26.8 %copy-start.30 = (f32[512]{0:T(512)S(1)}, f32[512]{0:T(512)}, u32[]{:S(2)}) copy-start(f32[512]{0:T(512)} %dynamic-slice_convert_fusion) | copy-start | bytes 6148
  280.3 26.8 %copy-start.33 = (f32[768]{0:T(1024)S(1)}, f32[768]{0:T(1024)}, u32[]{:S(2)}) copy-start(f32[768]{0:T(1024)} %get-tuple-element.313) | copy-start | bytes 9220
  280.3 26.8 %copy-start.35 = (f32[512]{0:T(512)S(1)}, f32[512]{0:T(512)}, u32[]{:S(2)}) copy-start(f32[512]{0:T(512)} %copy-done.34) | copy-start | bytes 6148
  280.3 26.8 %copy-start.40 = (f32[512]{0:T(512)S(1)}, f32[512]{0:T(512)}, u32[]{:S(2)}) copy-start(f32[512]{0:T(512)} %copy-done.39) | copy-start | bytes 6148
  280.3 29.5 %copy-start.44 = (f32[512]{0:T(512)S(1)}, f32[512]{0:T(512)}, u32[]{:S(2)}) copy-start(f32[512]{0:T(512)} %copy-done.43) | copy-start | bytes 6148
  280.3 67.0 %copy-start.46 = (f32[768]{0:T(1024)S(1)}, f32[768]{0:T(1024)}, u32[]{:S(2)}) copy-start(f32[768]{0:T(1024)} %get-tuple-element.230) | copy-start | bytes 9220
  280.4 102.2 %all-gather.11.cloned.1.call-start = ((), (), s32[]{:S(2)}) async-start(), calls=%async_computation.14 | async-start | bytes 3932160 | tf_op jit(solution)/shard_map/all_gather | solution.py:177
  309.8 42.1 %copy-start.15 = (bf16[512,768]{1,0:T(8,128)(2,1)S(1)}, bf16[512,768]{1,0:T(8,128)(2,1)}, u32[]{:S(2)}) copy-start(bf16[512,768]{1,0:T(8,128)(2,1)} %param.27) | copy-start | bytes 2359300
  350.7 31.9 %copy-start.18 = (bf16[4,24,8,512]{3,2,0,1:T(8,128)(2,1)S(1)}, bf16[4,24,8,512]{3,2,0,1:T(8,128)(2,1)}, u32[]{:S(2)}) copy-start(bf16[4,24,8,512]{3,2,0,1:T(8,128)(2,1)} %copy-done.17) | copy-start | bytes 2359300
  350.7 36.0 %copy-start.41 = (f32[512]{0:T(512)}, f32[512]{0:T(512)S(1)}, u32[]{:S(2)}) copy-start(f32[512]{0:T(512)S(1)} %negate_multiply_fusion.2) | copy-start | bytes 6148
  353.9 221.0 %reduce-scatter.25.cloned.1.call-start = ((), (), s32[]{:S(2)}) async-start(), calls=%async_computation.19 | async-start | bytes 884736
  354.0 32.8 %copy-start.24 = (bf16[192,768]{1,0:T(8,128)(2,1)S(1)}, bf16[192,768]{1,0:T(8,128)(2,1)}, u32[]{:S(2)}) copy-start(bf16[192,768]{1,0:T(8,128)(2,1)} %param.22) | copy-start | bytes 884740
  386.7 197.1 %reduce-scatter.17.cloned.1.call-start = ((), (), s32[]{:S(2)}) async-start(), calls=%async_computation.15 | async-start | bytes 3932160 | tf_op jit(solution)/shard_map/reduce_scatter | solution.py:237
  545.8 112.2 %reduce-scatter.23.cloned.1.call-start = ((), (), s32[]{:S(2)}) async-start(), calls=%async_computation.18 | async-start | bytes 2654208 | tf_op jit(solution)/shard_map/reduce_scatter | solution.py:268
  552.8 178.1 %reduce-scatter.21.cloned.1.call-start = ((), (), s32[]{:S(2)}) async-start(), calls=%async_computation.17 | async-start | bytes 2654208 | tf_op jit(solution)/shard_map/reduce_scatter | solution.py:267
  560.7 243.1 %reduce-scatter.19.cloned.1.call-start = ((), (), s32[]{:S(2)}) async-start(), calls=%async_computation.16 | async-start | bytes 2654208 | tf_op jit(solution)/shard_map/reduce_scatter | solution.py:265
  567.1 65.5 %copy-start.13 = (f32[512,768]{1,0:T(8,128)S(1)}, f32[512,768]{1,0:T(8,128)}, u32[]{:S(2)}) copy-start(f32[512,768]{1,0:T(8,128)} %copy-done.12) | copy-start | bytes 4718596
  585.5 218.3 %copy-start.1 = (bf16[768,768]{1,0:T(8,128)(2,1)S(1)}, bf16[768,768]{1,0:T(8,128)(2,1)}, u32[]{:S(2)}) copy-start(bf16[768,768]{1,0:T(8,128)(2,1)} %param.26) | copy-start | bytes 3538948
  (51 other events, 246.8 us)
Sparse Core Ops, SparseCore 0:
  14.8 31.2 all-gather.4
  139.1 37.8 reduce-scatter.10
  184.1 28.4 all-gather.6
  214.6 28.4 all-gather.8
  269.1 37.8 reduce-scatter.14
  309.5 37.8 reduce-scatter.12
  354.0 28.4 all-gather.10
  386.8 63.2 reduce-scatter.24
  545.9 37.8 reduce-scatter.16
  587.7 70.1 reduce-scatter.22
  662.0 68.8 reduce-scatter.20
  734.8 68.9 reduce-scatter.18
where the time goes:
time: 816 us; the launch traced here: 811 us
  waiting for transfers between devices  383 us (47%)
  matrix products  195 us (24%)
  other arithmetic  106 us (13%)
  local copies, waits for them, and re-layouts  52.8 us (6%)
  blocking collectives  41.6 us (5%)
  between operations  17.1 us (2%)
  loops' own time  14 us (2%)
    reduce_scatter x1, waiting for transfers between devices, on_device(): lax.psum_scatter(w_up_grad, 'dp', scatter_dimension=0, tiled=True)  72.9 us
    reduce_scatter x1, waiting for transfers between devices, on_device(): lax.psum_scatter(w_qkv_grad, 'dp', scatter_dimension=0, tiled=True)  72.9 us
    dot_general x8, matrix products, block_scores(): jnp.einsum('qhe,khe->hqk', query_block, key_heads, preferred_element_type...  49.1 us
    psum x1, blocking collectives, on_device(): lax.psum((jnp.stack([gain_one_grad, gain_two_grad]), jnp.stack([shift_one...  41.6 us
    reduce_scatter x1, waiting for transfers between devices, on_device(): lax.psum_scatter(jnp.dot(hidden, w_down, preferred_element_type=jnp.float...  37.6 us
    reduce_scatter x1, waiting for transfers between devices, on_device(): lax.psum_scatter(jnp.dot(mixed_rows, w_out, preferred_element_type=jnp.fl...  36.2 us
    all_gather x1, waiting for transfers between devices, on_device(): attn_grad = lax.all_gather(attn_local, 'tensor', axis=0, tiled=True)  28.6 us
    all_gather x1, waiting for transfers between devices, on_device(): normed_two = lax.all_gather(normed_two_local, 'tensor', axis=0, tiled=True)  28 us
  transfers between devices with their start and end apart: 12, of which 11 were waited for; matrix products, arithmetic and copies ran while one was open for 26% of the time, Pallas kernels for 0%

commit v1 on v0

--- a/solution.py
+++ b/solution.py
@@ -1,3 +1,5 @@
+import functools
+
 import jax
 import jax.numpy as jnp
 from jax import lax
@@ -60,7 +62,16 @@
     return jnp.sqrt(delta_row * delta_row + delta_col * delta_col)
 
 
+def scatter_rows(parts, dp_size):
+    width = parts.shape[1]
+    padded = -(-width // 1024) * 1024
+    parts = jnp.pad(parts, ((0, 0), (0, padded - width))).reshape(dp_size * padded // 128, 128)
+    summed = lax.psum_scatter(parts, "dp", scatter_dimension=0, tiled=True)
+    return summed.reshape(-1)[:width]
+
+
 def on_device(
+    dp_size,
     patches,
     counts,
     norm_gain,
@@ -155,7 +166,9 @@
     branch_grad = lax.all_gather(
         (keep_rows * upstream).astype(jnp.bfloat16), "tensor", axis=0, tiled=True
     )
-    w_down_grad = jnp.einsum("tf,td->fd", hidden, branch_grad, preferred_element_type=jnp.float32)
+    w_down_grad_t = jnp.einsum(
+        "td,tf->df", branch_grad, hidden, preferred_element_type=jnp.float32
+    )
     hidden_grad = jnp.einsum("td,fd->tf", branch_grad, w_down, preferred_element_type=jnp.float32)
     _, gelu_back = jax.vjp(lambda pre_act: jax.nn.gelu(pre_act, approximate=False), hidden_pre)
     pre_grad = gelu_back(hidden_grad)[0].astype(jnp.bfloat16)
@@ -175,10 +188,22 @@
     attn_bias_grad = jnp.sum(keep_rows * after_grad, axis=0)
     attn_local = (keep_rows * after_grad).astype(jnp.bfloat16)
     attn_grad = lax.all_gather(attn_local, "tensor", axis=0, tiled=True)
-    w_out_grad = jnp.einsum("tc,td->cd", mixed_rows, attn_grad, preferred_element_type=jnp.float32)
+    w_out_grad_t = jnp.einsum(
+        "td,tc->dc", attn_grad, mixed_rows, preferred_element_type=jnp.float32
+    )
     mixed_grad = jnp.einsum(
         "td,cd->tc", attn_grad, w_out, preferred_element_type=jnp.float32
     ).astype(jnp.bfloat16)
+    early_parts = jnp.concatenate(
+        [
+            w_down_grad_t.reshape(dp_size, -1),
+            w_up_grad.reshape(dp_size, -1),
+            w_out_grad_t.reshape(dp_size, -1),
+        ],
+        axis=1,
+    )
+    early_parts, mixed_grad = lax.optimization_barrier((early_parts, mixed_grad))
+    early_sum = scatter_rows(early_parts, dp_size)
     mixed_heads = mixed_grad.reshape(TOK_DEV, heads_here, HEAD_DIM)
 
     def back_block(running, block_index):
@@ -218,9 +243,15 @@
         )
 
     zero_heads = jnp.zeros((TOK_DEV, heads_here, HEAD_DIM), jnp.float32)
-    (key_acc, value_acc), query_blocks = lax.scan(
-        back_block, (zero_heads, zero_heads), jnp.arange(block_count, dtype=jnp.int32)
-    )
+    half_count = block_count // 2
+    running, query_first = lax.scan(
+        back_block, (zero_heads, zero_heads), jnp.arange(half_count, dtype=jnp.int32)
+    )
+    running, early_sum = lax.optimization_barrier((running, early_sum))
+    (key_acc, value_acc), query_second = lax.scan(
+        back_block, running, jnp.arange(half_count, block_count, dtype=jnp.int32)
+    )
+    query_blocks = jnp.concatenate([query_first, query_second], axis=0)
     query_grad = query_blocks.reshape(TOK_DEV, width_here)
     key_grad = key_acc.reshape(TOK_DEV, width_here).astype(jnp.bfloat16)
     value_grad = value_acc.reshape(TOK_DEV, width_here).astype(jnp.bfloat16)
@@ -242,31 +273,44 @@
         scatter_dimension=0,
         tiled=True,
     ).astype(jnp.float32)
-    qv_full = lax.dynamic_update_slice_in_dim(
-        jnp.zeros((2, D), jnp.float32), qv_bias_grad, tensor_pos * width_here, 1
-    )
     _, norm_one_back = jax.vjp(normalize, inputs, norm_gain[0], norm_bias[0])
     through_one, gain_one_grad, shift_one_grad = norm_one_back(normed_grad)
     input_grad = (after_grad + through_one).astype(jnp.bfloat16)
-    up_full = lax.dynamic_update_slice_in_dim(
-        jnp.zeros((FF,), jnp.float32), up_bias_grad, tensor_pos * ff_here, 0
-    )
-    gains_grad, shifts_grad, outer_grad, qv_sum, up_sum = lax.psum(
-        (
-            jnp.stack([gain_one_grad, gain_two_grad]),
-            jnp.stack([shift_one_grad, shift_two_grad]),
-            jnp.stack([attn_bias_grad, down_bias_grad]),
-            qv_full,
-            up_full,
-        ),
-        ("dp", "tensor"),
-    )
-    qkv_part, out_part, up_part, down_part = (
-        lax.psum_scatter(w_qkv_grad, "dp", scatter_dimension=0, tiled=True),
-        lax.psum_scatter(w_out_grad, "dp", scatter_dimension=1, tiled=True),
-        lax.psum_scatter(w_up_grad, "dp", scatter_dimension=0, tiled=True),
-        lax.psum_scatter(w_down_grad, "dp", scatter_dimension=1, tiled=True),
-    )
+    small = jnp.concatenate(
+        [
+            jnp.stack([gain_one_grad, gain_two_grad]).reshape(-1),
+            jnp.stack([shift_one_grad, shift_two_grad]).reshape(-1),
+            jnp.stack([attn_bias_grad, down_bias_grad]).reshape(-1),
+            qv_bias_grad.reshape(-1),
+            up_bias_grad,
+        ]
+    )
+    late_parts = jnp.concatenate(
+        [w_qkv_grad.reshape(dp_size, -1), jnp.broadcast_to(small, (dp_size,) + small.shape)],
+        axis=1,
+    )
+    late_sum = scatter_rows(late_parts, dp_size)
+    qkv_size = w_qkv_grad.size // dp_size
+    rows_dp = D // dp_size
+    qkv_part = late_sum[:qkv_size].reshape(rows_dp, 3, width_here)
+    small_all = lax.all_gather(late_sum[qkv_size:], "tensor", axis=0, tiled=False)
+    tensor_size = small_all.shape[0]
+    summed = jnp.sum(small_all[:, : 6 * D], axis=0)
+    gains_grad = summed[: 2 * D].reshape(2, D)
+    shifts_grad = summed[2 * D : 4 * D].reshape(2, D)
+    outer_grad = summed[4 * D : 6 * D].reshape(2, D)
+    qv_sum = (
+        small_all[:, 6 * D : 6 * D + 2 * width_here]
+        .reshape(tensor_size, 2, width_here)
+        .transpose(1, 0, 2)
+        .reshape(2, D)
+    )
+    up_sum = small_all[:, 6 * D + 2 * width_here :].reshape(FF)
+    down_size = D * ff_here // dp_size
+    up_size = D * ff_here // dp_size
+    down_part = early_sum[:down_size].reshape(rows_dp, ff_here).T
+    up_part = early_sum[down_size : down_size + up_size].reshape(rows_dp, ff_here)
+    out_part = early_sum[down_size + up_size :].reshape(rows_dp, width_here).T
     return (
         result,
         input_grad,
@@ -298,7 +342,7 @@
         P(("dp", "tensor"), None),
     )
     return jax.shard_map(
-        on_device,
+        functools.partial(on_device, mesh.shape["dp"]),
         mesh=mesh,
         in_specs=placed,
         out_specs=(

time: 816 us -> 781 us (0.957)
  waiting for transfers between devices: 383 us -> 269 us
  matrix products: 195 us -> 238 us
  local copies, waits for them, and re-layouts: 52.8 us -> 94.3 us
  blocking collectives: 41.6 us -> 5.31 us
  other arithmetic: 106 us -> 137 us
    reduce_scatter x3 -> x2, waiting for transfers between devices: 168 us -> 59.2 us  [scatter_rows(): summed = lax.psum_scatter(parts, 'dp', scatter_dimension=0, tiled=True)]
    psum x1 -> x0, blocking collectives: 41.6 us -> none  [on_device(): lax.psum((jnp.stack([gain_one_grad, gain_two_grad]), jnp.stack([shift_one...]
    reshape x0 -> x15, local copies, waits for them, and re-layouts: none -> 24.9 us  [the longest x2 8.83 us: scatter_rows(): jnp.pad(parts, ((0, 0), (0, padded - width)))]
    all_gather x1, waiting for transfers between devices: 28.6 us -> 6.49 us  [on_device(): attn_grad = lax.all_gather(attn_local, 'tensor', axis=0, tiled=True)]
    dot_general x4, matrix products: 11.1 us -> 29.1 us  [back_block(): jnp.einsum('qhe,khe->hqk', grad_block, value_heads, preferred_element_typ...]
    reduce_scatter x1, waiting for transfers between devices: 7.29 us -> 24.4 us  [on_device(): lax.psum_scatter(jnp.einsum('tsc,dsc->td', projected_grad, w_qkv, preferr...]
    dot_general x8, matrix products: 49.1 us -> 65.6 us  [block_scores(): jnp.einsum('qhe,khe->hqk', query_block, key_heads, preferred_element_type...]
    convert_element_type x4, other arithmetic: 22.4 us -> 36.4 us  [back_block(): score_grad = (weights * (weight_grad - jnp.sum(weights * weight_grad, axi...]
  transfers between devices with their start and end apart: 12 -> 10, of which waited for: 11 -> 9; matrix products, arithmetic and copies ran while one was open for 26% -> 21% of each run, Pallas kernels for 0% -> 0%
where the time goes in v1:
time: 781 us; the launch traced here: 776 us
  waiting for transfers between devices  269 us (34%)
  matrix products  238 us (30%)
  other arithmetic  137 us (18%)
  local copies, waits for them, and re-layouts  94.3 us (12%)
  between operations  17.2 us (2%)
  loops' own time  13.9 us (2%)
    dot_general x8, matrix products, block_scores(): jnp.einsum('qhe,khe->hqk', query_block, key_heads, preferred_element_type...  65.6 us
    reduce_scatter x2, waiting for transfers between devices, scatter_rows(): summed = lax.psum_scatter(parts, 'dp', scatter_dimension=0, tiled=True)  59.2 us
    reduce_scatter x1, waiting for transfers between devices, on_device(): lax.psum_scatter(jnp.dot(hidden, w_down, preferred_element_type=jnp.float...  37.6 us
    reduce_scatter x1, waiting for transfers between devices, on_device(): lax.psum_scatter(jnp.dot(mixed_rows, w_out, preferred_element_type=jnp.fl...  36.5 us
    convert_element_type x4, other arithmetic, back_block(): score_grad = (weights * (weight_grad - jnp.sum(weights * weight_grad, axi...  36.4 us
    dot_general x4, matrix products, back_block(): jnp.einsum('qhe,khe->hqk', grad_block, value_heads, preferred_element_typ...  29.1 us
    all_gather x1, waiting for transfers between devices, on_device(): normed_two = lax.all_gather(normed_two_local, 'tensor', axis=0, tiled=True)  28 us
    all_gather x1, waiting for transfers between devices, on_device(): normed = lax.all_gather(normed_local, 'tensor', axis=0, tiled=True)  26.9 us
  transfers between devices with their start and end apart: 10, of which 9 were waited for; matrix products, arithmetic and copies ran while one was open for 21% of the time, Pallas kernels for 0%

profile of v1, /device:TPU:0, one launch (start us, length us, event | category | flops | bytes accessed | tf_op | source)
XLA Modules:
  0.0 775.6 jit_solution(12990185017323670892)
XLA Ops:
  19.7 26.9 %all-gather.6.cloned.1.call-done = bf16[2048,768]{1,0:T(8,128)(2,1)} async-done(((bf16[512,768]{1,0:T(8,128)(2,1)}), bf16[2048,768]{1,0:T(8,128)(2,1)}) %all-gather.6.cloned.1.call-update) | async-done | bytes 3145744 | tf_op jit(solution)/shard_map/all_gather | solution.py:100
  51.9 80.1 %while.43 = (s32[]{:T(128)}, bf16[4,512,192]{1,2,0:T(8,128)(2,1)}, f32[4,3,512]{2,1,0:T(4,128)}, s32[4]{0:T(128)}, s32[2048]{0:T(1024)S(1)}, /*index=5*/bf16[204...) while((s32[]{:T(128)}, bf16[4,512,192]{1,2,0:T(8,128)(2,1)}, ...), condition=%wide.region_5.6_spmd.clone, body=%wide.region_2.5_spmd.clone.sunk | while | flops 868317696 | bytes 61568268 | solution.py:144
  140.0 36.5 %reduce-scatter.7.cloned.1.call-done = bf16[512,768]{1,0:T(8,128)(2,1)} async-done(((bf16[2048,768]{1,0:T(8,128)(2,1)}), bf16[512,768]{1,0:T(8,128)(2,1)}) %reduce-scatter.7.cloned.1.call-update) | async-done | bytes 786448 | tf_op jit(solution)/shard_map/reduce_scatter | solution.py:146
  184.1 28.0 %all-gather.8.cloned.1.call-done = bf16[2048,768]{1,0:T(8,128)(2,1)} async-done(((bf16[512,768]{1,0:T(8,128)(2,1)}), bf16[2048,768]{1,0:T(8,128)(2,1)}) %all-gather.8.cloned.1.call-update) | async-done | bytes 3145744 | tf_op jit(solution)/shard_map/all_gather | solution.py:154
  212.1 7.5 fusion.90
  219.6 23.0 %all-gather.10.cloned.1.call-done = bf16[2048,768]{1,0:T(8,128)(2,1)} async-done(((bf16[512,768]{1,0:T(8,128)(2,1)}), bf16[2048,768]{1,0:T(8,128)(2,1)}) %all-gather.10.cloned.1.call-update) | async-done | bytes 3145744 | tf_op jit(solution)/shard_map/all_gather | solution.py:166
  242.7 20.2 %convert_reduce_fusion = (f32[768]{0:T(1024)}, bf16[2048,768]{1,0:T(8,128)(2,1)S(1)}, f32[2048,768]{1,0:T(8,128)}) fusion(f32[2048,768]{1,0:T(8,128)} %fusion.90, f32[768]{0:T(1024)} %param.27, bf16[2048,768]{1,0:T(8,128)(2,1)} %all-gather.10.cloned.1.call-done, bf16[768,768]{1,0:T(8,128)(2,1)S(1)} %copy-done), kind=kOutput, calls=%fused_computation.67 | convolution fusion | flops 2533883136 | bytes 20060160 | tf_op jit(solution)/shard_map/td,fd->tf/dot_general | solution.py:172
  280.3 26.3 %reduce-scatter.11.cloned.1.call-done = bf16[512,768]{1,0:T(8,128)(2,1)} async-done(((bf16[2048,768]{1,0:T(8,128)(2,1)}), bf16[512,768]{1,0:T(8,128)(2,1)}) %reduce-scatter.11.cloned.1.call-update) | async-done | bytes 786448 | tf_op jit(solution)/shard_map/reduce_scatter | solution.py:177
  309.4 37.6 %reduce-scatter.9.cloned.1.call-done = bf16[512,768]{1,0:T(8,128)(2,1)} async-done(((bf16[2048,768]{1,0:T(8,128)(2,1)}), bf16[512,768]{1,0:T(8,128)(2,1)}) %reduce-scatter.9.cloned.1.call-update) | async-done | bytes 786448 | tf_op jit(solution)/shard_map/reduce_scatter | solution.py:157
  354.0 7.0 fusion.91
  365.0 7.0 fusion.92
  375.6 6.5 all-gather.12.cloned.1.call-done
  387.4 6.5 pad_maximum_fusion
  395.9 5.7 reshape.588
  402.8 110.2 %while.45 = (s32[]{:T(128)}, f32[2048,3,64]{0,2,1:T(8,128)S(1)}, f32[2048,3,64]{0,2,1:T(8,128)}, bf16[2,512,192]{1,2,0:T(8,128)(2,1)}, s32[2]{0:T(128)S(1)}, /*i...) while((s32[]{:T(128)}, f32[2048,3,64]{0,2,1:T(8,128)S(1)}, ...), condition=%wide.region_15.16_spmd.clone, body=%wide.region_13.15_spmd.clone.sunk | while | flops 2056321536 | bytes 181412336 | solution.py:247
  407.8 7.3 fusion.199
  419.8 12.9 %multiply_reduce_fusion.7 = (f32[3,512]{1,0:T(4,128)S(1)}, f32[3,512,2048]{2,1,0:T(8,128)}) fusion(f32[3,512,2048]{2,1,0:T(8,128)} %fusion.199, f32[3,512]{1,0:T(4,128)S(1)} %dynamic-slice_bitcast_fusion.5, f32[512,2048]{1,0:T(8,128)} %add_sqrt_fusion.8, f32[3]{0:T(128)S(1)} %multiply_exponential_fusion.8, bf16[512,3,64]{0,2,1:T(8,128)(2,1)S(1)} %bitcast.189, ...), kind=kOutput, calls=%fused_computation.42.clone.1 | convolution fusion | flops 424671744 | bytes 31404044 | tf_op jit(solution)/shard_map/while/body/eval_jaxpr/qhe,khe->hqk/dot_general | solution.py:113
  434.5 8.5 %multiply_convert_fusion.7 = bf16[3,512,2048]{2,1,0:T(8,128)(2,1)} fusion(f32[3,512,2048]{2,1,0:T(8,128)} %get-tuple-element.743, f32[3,512,2048]{2,1,0:T(8,128)S(1)} %bitcast.185, f32[3,512]{1,0:T(4,128)S(1)} %get-tuple-element.744), kind=kLoop, calls=%fused_computation.41.clone.1 | loop fusion | flops 9437184 | bytes 31463424 | tf_op jit(solution)/shard_map/while/body/eval_jaxpr/convert_element_type | solution.py:228
  450.5 7.3 fusion.201
  462.8 7.3 fusion.199
  474.9 12.8 %multiply_reduce_fusion.7 = (f32[3,512]{1,0:T(4,128)S(1)}, f32[3,512,2048]{2,1,0:T(8,128)}) fusion(f32[3,512,2048]{2,1,0:T(8,128)} %fusion.199, f32[3,512]{1,0:T(4,128)S(1)} %dynamic-slice_bitcast_fusion.5, f32[512,2048]{1,0:T(8,128)} %add_sqrt_fusion.8, f32[3]{0:T(128)S(1)} %multiply_exponential_fusion.8, bf16[512,3,64]{0,2,1:T(8,128)(2,1)S(1)} %bitcast.189, ...), kind=kOutput, calls=%fused_computation.42.clone.1 | convolution fusion | flops 424671744 | bytes 31404044 | tf_op jit(solution)/shard_map/while/body/eval_jaxpr/qhe,khe->hqk/dot_general | solution.py:113
  489.6 8.4 %multiply_convert_fusion.7 = bf16[3,512,2048]{2,1,0:T(8,128)(2,1)} fusion(f32[3,512,2048]{2,1,0:T(8,128)} %get-tuple-element.743, f32[3,512,2048]{2,1,0:T(8,128)S(1)} %bitcast.185, f32[3,512]{1,0:T(4,128)S(1)} %get-tuple-element.744), kind=kLoop, calls=%fused_computation.41.clone.1 | loop fusion | flops 9437184 | bytes 31463424 | tf_op jit(solution)/shard_map/while/body/eval_jaxpr/convert_element_type | solution.py:228
  505.5 7.5 fusion.201
  515.5 110.5 %while.44 = (s32[]{:T(128)}, f32[2048,3,64]{0,2,1:T(8,128)S(1)}, f32[2048,3,64]{0,2,1:T(8,128)}, bf16[2,512,192]{1,2,0:T(8,128)(2,1)}, s32[2]{0:T(128)S(1)}, /*i...) while((s32[]{:T(128)}, f32[2048,3,64]{0,2,1:T(8,128)S(1)}, ...), condition=%wide.region_19.20_spmd.clone, body=%wide.region_17.19_spmd.clone.sunk | while | flops 2055535104 | bytes 193995312 | solution.py:247
  520.8 7.3 fusion.185
  532.8 12.8 %multiply_reduce_fusion.6 = (f32[3,512]{1,0:T(4,128)S(1)}, f32[3,512,2048]{2,1,0:T(8,128)}) fusion(f32[3,512,2048]{2,1,0:T(8,128)} %fusion.185, f32[3,512]{1,0:T(4,128)S(1)} %dynamic-slice_bitcast_fusion.4, f32[512,2048]{1,0:T(8,128)} %add_sqrt_fusion.7, f32[3]{0:T(128)S(1)} %multiply_exponential_fusion.7, bf16[512,3,64]{0,2,1:T(8,128)(2,1)S(1)} %bitcast.191, ...), kind=kOutput, calls=%fused_computation.19.clone.1 | convolution fusion | flops 424671744 | bytes 31404044 | tf_op jit(solution)/shard_map/while/body/eval_jaxpr/qhe,khe->hqk/dot_general | solution.py:113
  547.1 9.8 %multiply_convert_fusion.6 = bf16[3,512,2048]{2,1,0:T(8,128)(2,1)} fusion(f32[3,512,2048]{2,1,0:T(8,128)} %get-tuple-element.727, f32[3,512,2048]{2,1,0:T(8,128)S(1)} %bitcast.183, f32[3,512]{1,0:T(4,128)S(1)} %get-tuple-element.728), kind=kLoop, calls=%fused_computation.18.clone.1 | loop fusion | flops 9437184 | bytes 31463424 | tf_op jit(solution)/shard_map/while/body/eval_jaxpr/convert_element_type | solution.py:228
  575.9 7.3 fusion.185
  587.9 12.8 %multiply_reduce_fusion.6 = (f32[3,512]{1,0:T(4,128)S(1)}, f32[3,512,2048]{2,1,0:T(8,128)}) fusion(f32[3,512,2048]{2,1,0:T(8,128)} %fusion.185, f32[3,512]{1,0:T(4,128)S(1)} %dynamic-slice_bitcast_fusion.4, f32[512,2048]{1,0:T(8,128)} %add_sqrt_fusion.7, f32[3]{0:T(128)S(1)} %multiply_exponential_fusion.7, bf16[512,3,64]{0,2,1:T(8,128)(2,1)S(1)} %bitcast.191, ...), kind=kOutput, calls=%fused_computation.19.clone.1 | convolution fusion | flops 424671744 | bytes 31404044 | tf_op jit(solution)/shard_map/while/body/eval_jaxpr/qhe,khe->hqk/dot_general | solution.py:113
  602.2 9.8 %multiply_convert_fusion.6 = bf16[3,512,2048]{2,1,0:T(8,128)(2,1)} fusion(f32[3,512,2048]{2,1,0:T(8,128)} %get-tuple-element.727, f32[3,512,2048]{2,1,0:T(8,128)S(1)} %bitcast.183, f32[3,512]{1,0:T(4,128)S(1)} %get-tuple-element.728), kind=kLoop, calls=%fused_computation.18.clone.1 | loop fusion | flops 9437184 | bytes 31463424 | tf_op jit(solution)/shard_map/while/body/eval_jaxpr/convert_element_type | solution.py:228
  654.3 24.4 %reduce-scatter.15.cloned.1.call-done = bf16[512,768]{1,0:T(8,128)(2,1)} async-done(((bf16[2048,768]{1,0:T(8,128)(2,1)}), bf16[512,768]{1,0:T(8,128)(2,1)}) %reduce-scatter.15.cloned.1.call-update) | async-done | bytes 786448 | tf_op jit(solution)/shard_map/reduce_scatter | solution.py:268
  697.7 59.2 %reduce-scatter.17.cloned.1.call-done = f32[480,128]{1,0:T(8,128)} async-done(((f32[3840,128]{1,0:T(8,128)}), f32[480,128]{1,0:T(8,128)}) %reduce-scatter.17.cloned.1.call-update) | async-done | bytes 245776 | tf_op jit(solution)/shard_map/reduce_scatter | solution.py:69
  (415 shorter events, 290.6 us)
Async XLA Ops:
  7.2 235.5 %copy-start = (bf16[768,768]{1,0:T(8,128)(2,1)S(1)}, bf16[768,768]{1,0:T(8,128)(2,1)}, u32[]{:S(2)}) copy-start(bf16[768,768]{1,0:T(8,128)(2,1)} %param.28) | copy-start | bytes 3538948
  7.2 39.4 %copy-start.60 = (bf16[768,3,192]{0,2,1:T(8,128)(2,1)S(1)}, bf16[768,3,192]{0,2,1:T(8,128)(2,1)}, u32[]{:S(2)}) copy-start(bf16[768,3,192]{0,2,1:T(8,128)(2,1)} %param.22) | copy-start | bytes 2654212
  7.2 39.4 %all-gather.6.cloned.1.call-start = ((), (), s32[]{:S(2)}) async-start(), calls=%async_computation.6 | async-start | bytes 3932160 | tf_op jit(solution)/shard_map/all_gather | solution.py:100
  15.2 161.3 %reduce-scatter.7.cloned.1.call-start = ((), (), s32[]{:S(2)}) async-start(), calls=%async_computation.7 | async-start | bytes 3932160 | tf_op jit(solution)/shard_map/reduce_scatter | solution.py:146
  138.4 38.1 %copy-start.5 = (bf16[512,768]{1,0:T(8,128)(2,1)S(1)}, bf16[512,768]{1,0:T(8,128)(2,1)}, u32[]{:S(2)}) copy-start(bf16[512,768]{1,0:T(8,128)(2,1)} %param.18) | copy-start | bytes 2359300
  138.5 73.7 %all-gather.8.cloned.1.call-start = ((), (), s32[]{:S(2)}) async-start(), calls=%async_computation.8 | async-start | bytes 3932160 | tf_op jit(solution)/shard_map/all_gather | solution.py:154
  183.5 59.2 %all-gather.10.cloned.1.call-start = ((), (), s32[]{:S(2)}) async-start(), calls=%async_computation.10 | async-start | bytes 3932160 | tf_op jit(solution)/shard_map/all_gather | solution.py:166
  184.1 122.6 %reduce-scatter.11.cloned.1.call-start = ((), (), s32[]{:S(2)}) async-start(), calls=%async_computation.11 | async-start | bytes 3932160 | tf_op jit(solution)/shard_map/reduce_scatter | solution.py:177
  242.7 21.8 %copy-start.59 = (bf16[768,768]{1,0:T(8,128)(2,1)S(1)}, bf16[768,768]{1,0:T(8,128)(2,1)}, u32[]{:S(2)}) copy-start(bf16[768,768]{1,0:T(8,128)(2,1)} %param.26) | copy-start | bytes 3538948
  268.6 78.3 %reduce-scatter.9.cloned.1.call-start = ((), (), s32[]{:S(2)}) async-start(), calls=%async_computation.9 | async-start | bytes 3932160 | tf_op jit(solution)/shard_map/reduce_scatter | solution.py:157
  279.8 26.9 %copy-start.28 = (f32[768]{0:T(1024)S(1)}, f32[768]{0:T(1024)}, u32[]{:S(2)}) copy-start(f32[768]{0:T(1024)} %get-tuple-element.382) | copy-start | bytes 9220
  279.8 26.9 %copy-start.32 = (f32[512]{0:T(512)S(1)}, f32[512]{0:T(512)}, u32[]{:S(2)}) copy-start(f32[512]{0:T(512)} %dynamic-slice_convert_fusion) | copy-start | bytes 6148
  279.8 26.9 %copy-start.35 = (f32[768]{0:T(1024)S(1)}, f32[768]{0:T(1024)}, u32[]{:S(2)}) copy-start(f32[768]{0:T(1024)} %get-tuple-element.492) | copy-start | bytes 9220
  279.8 26.9 %copy-start.37 = (f32[512]{0:T(512)S(1)}, f32[512]{0:T(512)}, u32[]{:S(2)}) copy-start(f32[512]{0:T(512)} %copy-done.36) | copy-start | bytes 6148
  279.8 26.9 %copy-start.41 = (f32[512]{0:T(512)S(1)}, f32[512]{0:T(512)}, u32[]{:S(2)}) copy-start(f32[512]{0:T(512)} %copy-done.40) | copy-start | bytes 6148
  279.8 29.6 %copy-start.46 = (f32[512]{0:T(512)S(1)}, f32[512]{0:T(512)}, u32[]{:S(2)}) copy-start(f32[512]{0:T(512)} %copy-done.45) | copy-start | bytes 6148
  279.8 67.1 %copy-start.51 = (f32[768]{0:T(1024)S(1)}, f32[768]{0:T(1024)}, u32[]{:S(2)}) copy-start(f32[768]{0:T(1024)} %get-tuple-element.381) | copy-start | bytes 9220
  279.9 102.2 %all-gather.12.cloned.1.call-start = ((), (), s32[]{:S(2)}) async-start(), calls=%async_computation.12 | async-start | bytes 3932160 | tf_op jit(solution)/shard_map/all_gather | solution.py:190
  309.4 42.0 %copy-start.11 = (bf16[512,768]{1,0:T(8,128)(2,1)S(1)}, bf16[512,768]{1,0:T(8,128)(2,1)}, u32[]{:S(2)}) copy-start(bf16[512,768]{1,0:T(8,128)(2,1)} %param.29) | copy-start | bytes 2359300
  353.4 161.3 %reduce-scatter.13.cloned.1.call-start = ((), (), s32[]{:S(2)}) async-start(), calls=%async_computation.13 | async-start | bytes 5971968 | tf_op jit(solution)/shard_map/reduce_scatter | solution.py:69
  401.7 277.0 %reduce-scatter.15.cloned.1.call-start = ((), (), s32[]{:S(2)}) async-start(), calls=%async_computation.14 | async-start | bytes 3932160 | tf_op jit(solution)/shard_map/reduce_scatter | solution.py:268
  402.8 112.7 %copy-start.61 = (s32[2]{0:T(128)S(1)}, s32[2]{0:T(128)}, u32[]{:S(2)}) copy-start(s32[2]{0:T(128)} %iota_add_fusion) | copy-start | bytes 28
  602.2 19.8 %slice-start.6 = ((s8[12582912]{0:T(1024)(128)(4,1)}), s8[4194304]{0:T(1024)(128)(4,1)S(1)}, s32[]{:S(2)}) async-start(s8[12582912]{0:T(1024)(128)(4,1)} %bitcast.186), calls=%async_computation.22 | async-start | bytes 8388608 | tf_op jit(solution)/shard_map/while
  602.2 19.8 %slice-start.7 = ((s8[12582912]{0:T(1024)(128)(4,1)}), s8[4194304]{0:T(1024)(128)(4,1)S(1)}, s32[]{:S(2)}) async-start(s8[12582912]{0:T(1024)(128)(4,1)} %bitcast.186), calls=%async_computation.23 | async-start | bytes 8388608 | tf_op jit(solution)/shard_map/while
  640.9 116.1 %reduce-scatter.17.cloned.1.call-start = ((), (), s32[]{:S(2)}) async-start(), calls=%async_computation.15 | async-start | bytes 2211840 | tf_op jit(solution)/shard_map/reduce_scatter | solution.py:69
  649.1 29.6 %copy-start.6 = (bf16[512,768]{1,0:T(8,128)(2,1)S(1)}, bf16[512,768]{1,0:T(8,128)(2,1)}, u32[]{:S(2)}) copy-start(bf16[512,768]{1,0:T(8,128)(2,1)} %param.18) | copy-start | bytes 2359300
  649.1 29.6 %copy-start.30 = (f32[768]{0:T(1024)S(1)}, f32[768]{0:T(1024)}, u32[]{:S(2)}) copy-start(f32[768]{0:T(1024)} %copy-done.29) | copy-start | bytes 9220
  649.1 29.6 %copy-start.34 = (f32[512]{0:T(512)S(1)}, f32[512]{0:T(512)}, u32[]{:S(2)}) copy-start(f32[512]{0:T(512)} %copy-done.33) | copy-start | bytes 6148
  649.1 31.3 %copy-start.44 = (f32[512]{0:T(512)S(1)}, f32[512]{0:T(512)}, u32[]{:S(2)}) copy-start(f32[512]{0:T(512)} %copy-done.43) | copy-start | bytes 6148
  649.1 31.4 %copy-start.39 = (f32[512]{0:T(512)S(1)}, f32[512]{0:T(512)}, u32[]{:S(2)}) copy-start(f32[512]{0:T(512)} %copy-done.38) | copy-start | bytes 6148
  649.1 34.1 %copy-start.55 = (f32[768]{0:T(1024)S(1)}, f32[768]{0:T(1024)}, u32[]{:S(2)}) copy-start(f32[768]{0:T(1024)} %get-tuple-element.465) | copy-start | bytes 9220
  693.9 74.4 %copy-start.1 = (bf16[768,768]{1,0:T(8,128)(2,1)S(1)}, bf16[768,768]{1,0:T(8,128)(2,1)}, u32[]{:S(2)}) copy-start(bf16[768,768]{1,0:T(8,128)(2,1)} %param.28) | copy-start | bytes 3538948
  (64 other events, 365.5 us)
Sparse Core Ops, SparseCore 0:
  15.3 31.2 all-gather.5
  138.6 37.8 reduce-scatter.6
  183.6 28.4 all-gather.7
  214.1 28.4 all-gather.9
  268.8 37.8 reduce-scatter.10
  309.1 37.8 reduce-scatter.8
  353.6 28.4 all-gather.11
  401.8 104.4 reduce-scatter.12
  641.0 37.6 reduce-scatter.14
  689.6 67.3 reduce-scatter.16

commit v2 on v1

--- a/solution.py
+++ b/solution.py
@@ -142,6 +142,13 @@
         )
 
     mixed_blocks, log_totals = lax.map(attend_block, jnp.arange(block_count, dtype=jnp.int32))
+    upstream = cotangent.astype(jnp.float32)
+    branch_grad = lax.all_gather(
+        (keep_rows * upstream).astype(jnp.bfloat16), "tensor", axis=0, tiled=True
+    )
+    mixed_blocks, log_totals, branch_grad = lax.optimization_barrier(
+        (mixed_blocks, log_totals, branch_grad)
+    )
     mixed_rows = mixed_blocks.reshape(TOK_DEV, width_here)
     attended = lax.psum_scatter(
         jnp.dot(mixed_rows, w_out, preferred_element_type=jnp.float32).astype(jnp.bfloat16),
@@ -154,18 +161,10 @@
     normed_two = lax.all_gather(normed_two_local, "tensor", axis=0, tiled=True)
     hidden_pre = jnp.dot(normed_two, w_up, preferred_element_type=jnp.float32) + b_up
     hidden = jax.nn.gelu(hidden_pre, approximate=False).astype(jnp.bfloat16)
-    branch = lax.psum_scatter(
-        jnp.dot(hidden, w_down, preferred_element_type=jnp.float32).astype(jnp.bfloat16),
-        "tensor",
-        scatter_dimension=0,
-        tiled=True,
-    ).astype(jnp.float32)
-    result = (after_attn + keep_rows * (branch + out_bias[1])).astype(jnp.bfloat16)
-    upstream = cotangent.astype(jnp.float32)
+    branch_partial = jnp.dot(hidden, w_down, preferred_element_type=jnp.float32).astype(
+        jnp.bfloat16
+    )
     down_bias_grad = jnp.sum(keep_rows * upstream, axis=0)
-    branch_grad = lax.all_gather(
-        (keep_rows * upstream).astype(jnp.bfloat16), "tensor", axis=0, tiled=True
-    )
     w_down_grad_t = jnp.einsum(
         "td,tf->df", branch_grad, hidden, preferred_element_type=jnp.float32
     )
@@ -202,7 +201,13 @@
         ],
         axis=1,
     )
-    early_parts, mixed_grad = lax.optimization_barrier((early_parts, mixed_grad))
+    early_parts, mixed_grad, branch_partial = lax.optimization_barrier(
+        (early_parts, mixed_grad, branch_partial)
+    )
+    branch = lax.psum_scatter(branch_partial, "tensor", scatter_dimension=0, tiled=True).astype(
+        jnp.float32
+    )
+    result = (after_attn + keep_rows * (branch + out_bias[1])).astype(jnp.bfloat16)
     early_sum = scatter_rows(early_parts, dp_size)
     mixed_heads = mixed_grad.reshape(TOK_DEV, heads_here, HEAD_DIM)
 
@@ -243,15 +248,12 @@
         )
 
     zero_heads = jnp.zeros((TOK_DEV, heads_here, HEAD_DIM), jnp.float32)
-    half_count = block_count // 2
-    running, query_first = lax.scan(
-        back_block, (zero_heads, zero_heads), jnp.arange(half_count, dtype=jnp.int32)
-    )
-    running, early_sum = lax.optimization_barrier((running, early_sum))
-    (key_acc, value_acc), query_second = lax.scan(
-        back_block, running, jnp.arange(half_count, block_count, dtype=jnp.int32)
-    )
-    query_blocks = jnp.concatenate([query_first, query_second], axis=0)
+    (key_acc, value_acc), query_blocks = lax.scan(
+        back_block, (zero_heads, zero_heads), jnp.arange(block_count, dtype=jnp.int32)
+    )
+    key_acc, value_acc, query_blocks, early_sum, result = lax.optimization_barrier(
+        (key_acc, value_acc, query_blocks, early_sum, result)
+    )
     query_grad = query_blocks.reshape(TOK_DEV, width_here)
     key_grad = key_acc.reshape(TOK_DEV, width_here).astype(jnp.bfloat16)
     value_grad = value_acc.reshape(TOK_DEV, width_here).astype(jnp.bfloat16)

time: 781 us -> 718 us (0.919)
  waiting for transfers between devices: 269 us -> 209 us
    reduce_scatter x1, waiting for transfers between devices: 37.6 us -> 0.01 us  [on_device(): lax.psum_scatter(branch_partial, 'tensor', scatter_dimension=0, tiled=True)]
    all_gather x1, waiting for transfers between devices: 23 us -> 0.01 us  [on_device(): lax.all_gather((keep_rows * upstream).astype(jnp.bfloat16), 'tensor', axi...]
    reduce_scatter x1, waiting for transfers between devices: 26.3 us -> 38 us  [on_device(): lax.psum_scatter(jnp.einsum('tf,df->td', pre_grad, w_up, preferred_elemen...]
  transfers between devices with their start and end apart: 10 -> 10, of which waited for: 9 -> 6; matrix products, arithmetic and copies ran while one was open for 21% -> 50% of each run, Pallas kernels for 0% -> 0%
where the time goes in v2:
time: 718 us; the launch traced here: 712 us
  matrix products  237 us (33%)
  waiting for transfers between devices  209 us (29%)
  other arithmetic  134 us (19%)
  local copies, waits for them, and re-layouts  94.7 us (13%)
  between operations  17 us (2%)
  loops' own time  14.3 us (2%)
    dot_general x8, matrix products, block_scores(): jnp.einsum('qhe,khe->hqk', query_block, key_heads, preferred_element_type...  65.1 us
    reduce_scatter x2, waiting for transfers between devices, scatter_rows(): summed = lax.psum_scatter(parts, 'dp', scatter_dimension=0, tiled=True)  59.4 us
    reduce_scatter x1, waiting for transfers between devices, on_device(): lax.psum_scatter(jnp.einsum('tf,df->td', pre_grad, w_up, preferred_elemen...  38 us
    reduce_scatter x1, waiting for transfers between devices, on_device(): lax.psum_scatter(jnp.dot(mixed_rows, w_out, preferred_element_type=jnp.fl...  36.4 us
    convert_element_type x4, other arithmetic, back_block(): score_grad = (weights * (weight_grad - jnp.sum(weights * weight_grad, axi...  33.5 us
    dot_general x4, matrix products, back_block(): jnp.einsum('hqk,qhe->khe', weights.astype(jnp.bfloat16), grad_block, pref...  29.9 us
    all_gather x1, waiting for transfers between devices, on_device(): normed_two = lax.all_gather(normed_two_local, 'tensor', axis=0, tiled=True)  28.6 us
    dot_general x4, matrix products, back_block(): jnp.einsum('qhe,khe->hqk', grad_block, value_heads, preferred_element_typ...  25.5 us
  transfers between devices with their start and end apart: 10, of which 6 were waited for; matrix products, arithmetic and copies ran while one was open for 50% of the time, Pallas kernels for 0%

profile of v2, /device:TPU:0, one launch (start us, length us, event | category | flops | bytes accessed | tf_op | source)
XLA Modules:
  0.0 712.5 jit_solution(9427704774979982664)
XLA Ops:
  21.5 25.1 %all-gather.6.cloned.1.call-done = bf16[2048,768]{1,0:T(8,128)(2,1)} async-done(((bf16[512,768]{1,0:T(8,128)(2,1)}), bf16[2048,768]{1,0:T(8,128)(2,1)}) %all-gather.6.cloned.1.call-update) | async-done | bytes 3145744 | tf_op jit(solution)/shard_map/all_gather | solution.py:100
  53.0 80.5 %while.28 = (s32[]{:T(128)}, bf16[4,512,192]{1,2,0:T(8,128)(2,1)}, f32[4,3,512]{2,1,0:T(4,128)}, s32[4]{0:T(128)}, s32[2048]{0:T(1024)S(1)}, /*index=5*/bf16[204...) while((s32[]{:T(128)}, bf16[4,512,192]{1,2,0:T(8,128)(2,1)}, ...), condition=%wide.region_5.6_spmd.clone, body=%wide.region_2.5_spmd.clone.sunk | while | flops 868317696 | bytes 61568268 | solution.py:144
  141.2 36.4 %reduce-scatter.7.cloned.1.call-done = bf16[512,768]{1,0:T(8,128)(2,1)} async-done(((bf16[2048,768]{1,0:T(8,128)(2,1)}), bf16[512,768]{1,0:T(8,128)(2,1)}) %reduce-scatter.7.cloned.1.call-update) | async-done | bytes 786448 | tf_op jit(solution)/shard_map/reduce_scatter | solution.py:153
  183.8 28.6 %all-gather.10.cloned.1.call-done = bf16[2048,768]{1,0:T(8,128)(2,1)} async-done(((bf16[512,768]{1,0:T(8,128)(2,1)}), bf16[2048,768]{1,0:T(8,128)(2,1)}) %all-gather.10.cloned.1.call-update) | async-done | bytes 3145744 | tf_op jit(solution)/shard_map/all_gather | solution.py:161
  217.5 19.2 %convert_reduce_fusion = (f32[768]{0:T(1024)}, bf16[2048,768]{1,0:T(8,128)(2,1)S(1)}, f32[2048,768]{1,0:T(8,128)}) fusion(f32[2048,768]{1,0:T(8,128)S(1)} %fusion.72, f32[768]{0:T(1024)S(1)} %copy-done.52, bf16[2048,768]{1,0:T(8,128)(2,1)S(1)} %copy-done.57, bf16[768,768]{1,0:T(8,128)(2,1)S(1)} %copy-done), kind=kOutput, calls=%fused_computation.43 | convolution fusion | flops 2533883136 | bytes 20060160 | tf_op jit(solution)/shard_map/td,fd->tf/dot_general | solution.py:171
  242.5 38.0 %reduce-scatter.9.cloned.1.call-done = bf16[512,768]{1,0:T(8,128)(2,1)} async-done(((bf16[2048,768]{1,0:T(8,128)(2,1)}), bf16[512,768]{1,0:T(8,128)(2,1)}) %reduce-scatter.9.cloned.1.call-update) | async-done | bytes 786448 | tf_op jit(solution)/shard_map/reduce_scatter | solution.py:176
  305.3 6.9 fusion.74
  315.7 6.2 convolution_convert_fusion
  325.2 6.5 pad_maximum_fusion
  339.7 221.3 %while.29 = (s32[]{:T(128)}, f32[2048,3,64]{0,2,1:T(8,128)}, f32[2048,3,64]{0,2,1:T(8,128)}, bf16[4,512,192]{1,2,0:T(8,128)(2,1)}, s32[4]{0:T(128)S(1)}, /*index...) while((s32[]{:T(128)}, f32[2048,3,64]{0,2,1:T(8,128)}, ...), condition=%wide.region_14.15_spmd.clone, body=%wide.region_12.14_spmd.clone.sunk | while | flops 2056321536 | bytes 185345040 | solution.py:251
  345.4 6.5 fusion.146
  357.0 12.7 %multiply_reduce_fusion.4 = (f32[3,512]{1,0:T(4,128)S(1)}, f32[3,512,2048]{2,1,0:T(8,128)}) fusion(f32[3,512,2048]{2,1,0:T(8,128)} %fusion.146, f32[3,512]{1,0:T(4,128)S(1)} %dynamic-slice_bitcast_fusion.2, f32[512,2048]{1,0:T(8,128)} %add_sqrt_fusion.5, f32[3]{0:T(128)S(1)} %multiply_exponential_fusion.5, bf16[512,3,64]{0,2,1:T(8,128)(2,1)} %bitcast.135, ...), kind=kOutput, calls=%fused_computation.18.clone.1 | convolution fusion | flops 424671744 | bytes 31404044 | tf_op jit(solution)/shard_map/while/body/eval_jaxpr/qhe,khe->hqk/dot_general | solution.py:113
  371.1 8.4 %multiply_convert_fusion.4 = bf16[3,512,2048]{2,1,0:T(8,128)(2,1)} fusion(f32[3,512,2048]{2,1,0:T(8,128)} %get-tuple-element.525, f32[3,512,2048]{2,1,0:T(8,128)S(1)} %bitcast.133, f32[3,512]{1,0:T(4,128)S(1)} %get-tuple-element.526), kind=kLoop, calls=%fused_computation.17.clone.1 | loop fusion | flops 9437184 | bytes 31463424 | tf_op jit(solution)/shard_map/while/body/eval_jaxpr/convert_element_type | solution.py:233
  379.5 5.8 fusion.147
  388.1 7.2 %fusion.148 = f32[2048,3,64]{0,2,1:T(8,128)} fusion(f32[3,512,2048]{2,1,0:T(8,128)} %get-tuple-element.525, f32[2048,3,64]{0,2,1:T(8,128)} %get-tuple-element.593, pred[]{:T(512)S(6)} %compare.4, bf16[2048,3,64]{0,2,1:T(8,128)(2,1)} %copy-done.17, s32[]{:T(128)S(6)} %select_n.304), kind=kOutput, calls=%fused_computation.27.clone.1 | convolution fusion | flops 406585344 | bytes 15925253 | tf_op jit(solution)/shard_map/while/body/eval_jaxpr/hqk,qhe->khe/dot_general | solution.py:222
  400.4 6.3 fusion.146
  411.8 12.7 %multiply_reduce_fusion.4 = (f32[3,512]{1,0:T(4,128)S(1)}, f32[3,512,2048]{2,1,0:T(8,128)}) fusion(f32[3,512,2048]{2,1,0:T(8,128)} %fusion.146, f32[3,512]{1,0:T(4,128)S(1)} %dynamic-slice_bitcast_fusion.2, f32[512,2048]{1,0:T(8,128)} %add_sqrt_fusion.5, f32[3]{0:T(128)S(1)} %multiply_exponential_fusion.5, bf16[512,3,64]{0,2,1:T(8,128)(2,1)} %bitcast.135, ...), kind=kOutput, calls=%fused_computation.18.clone.1 | convolution fusion | flops 424671744 | bytes 31404044 | tf_op jit(solution)/shard_map/while/body/eval_jaxpr/qhe,khe->hqk/dot_general | solution.py:113
  426.1 8.5 %multiply_convert_fusion.4 = bf16[3,512,2048]{2,1,0:T(8,128)(2,1)} fusion(f32[3,512,2048]{2,1,0:T(8,128)} %get-tuple-element.525, f32[3,512,2048]{2,1,0:T(8,128)S(1)} %bitcast.133, f32[3,512]{1,0:T(4,128)S(1)} %get-tuple-element.526), kind=kLoop, calls=%fused_computation.17.clone.1 | loop fusion | flops 9437184 | bytes 31463424 | tf_op jit(solution)/shard_map/while/body/eval_jaxpr/convert_element_type | solution.py:233
  434.6 6.0 fusion.147
  443.3 7.6 %fusion.148 = f32[2048,3,64]{0,2,1:T(8,128)} fusion(f32[3,512,2048]{2,1,0:T(8,128)} %get-tuple-element.525, f32[2048,3,64]{0,2,1:T(8,128)} %get-tuple-element.593, pred[]{:T(512)S(6)} %compare.4, bf16[2048,3,64]{0,2,1:T(8,128)(2,1)} %copy-done.17, s32[]{:T(128)S(6)} %select_n.304), kind=kOutput, calls=%fused_computation.27.clone.1 | convolution fusion | flops 406585344 | bytes 15925253 | tf_op jit(solution)/shard_map/while/body/eval_jaxpr/hqk,qhe->khe/dot_general | solution.py:222
  456.1 6.3 fusion.146
  467.4 12.7 %multiply_reduce_fusion.4 = (f32[3,512]{1,0:T(4,128)S(1)}, f32[3,512,2048]{2,1,0:T(8,128)}) fusion(f32[3,512,2048]{2,1,0:T(8,128)} %fusion.146, f32[3,512]{1,0:T(4,128)S(1)} %dynamic-slice_bitcast_fusion.2, f32[512,2048]{1,0:T(8,128)} %add_sqrt_fusion.5, f32[3]{0:T(128)S(1)} %multiply_exponential_fusion.5, bf16[512,3,64]{0,2,1:T(8,128)(2,1)} %bitcast.135, ...), kind=kOutput, calls=%fused_computation.18.clone.1 | convolution fusion | flops 424671744 | bytes 31404044 | tf_op jit(solution)/shard_map/while/body/eval_jaxpr/qhe,khe->hqk/dot_general | solution.py:113
  481.6 8.4 %multiply_convert_fusion.4 = bf16[3,512,2048]{2,1,0:T(8,128)(2,1)} fusion(f32[3,512,2048]{2,1,0:T(8,128)} %get-tuple-element.525, f32[3,512,2048]{2,1,0:T(8,128)S(1)} %bitcast.133, f32[3,512]{1,0:T(4,128)S(1)} %get-tuple-element.526), kind=kLoop, calls=%fused_computation.17.clone.1 | loop fusion | flops 9437184 | bytes 31463424 | tf_op jit(solution)/shard_map/while/body/eval_jaxpr/convert_element_type | solution.py:233
  498.5 7.5 %fusion.148 = f32[2048,3,64]{0,2,1:T(8,128)} fusion(f32[3,512,2048]{2,1,0:T(8,128)} %get-tuple-element.525, f32[2048,3,64]{0,2,1:T(8,128)} %get-tuple-element.593, pred[]{:T(512)S(6)} %compare.4, bf16[2048,3,64]{0,2,1:T(8,128)(2,1)} %copy-done.17, s32[]{:T(128)S(6)} %select_n.304), kind=kOutput, calls=%fused_computation.27.clone.1 | convolution fusion | flops 406585344 | bytes 15925253 | tf_op jit(solution)/shard_map/while/body/eval_jaxpr/hqk,qhe->khe/dot_general | solution.py:222
  511.2 6.3 fusion.146
  522.6 12.6 %multiply_reduce_fusion.4 = (f32[3,512]{1,0:T(4,128)S(1)}, f32[3,512,2048]{2,1,0:T(8,128)}) fusion(f32[3,512,2048]{2,1,0:T(8,128)} %fusion.146, f32[3,512]{1,0:T(4,128)S(1)} %dynamic-slice_bitcast_fusion.2, f32[512,2048]{1,0:T(8,128)} %add_sqrt_fusion.5, f32[3]{0:T(128)S(1)} %multiply_exponential_fusion.5, bf16[512,3,64]{0,2,1:T(8,128)(2,1)} %bitcast.135, ...), kind=kOutput, calls=%fused_computation.18.clone.1 | convolution fusion | flops 424671744 | bytes 31404044 | tf_op jit(solution)/shard_map/while/body/eval_jaxpr/qhe,khe->hqk/dot_general | solution.py:113
  536.6 8.4 %multiply_convert_fusion.4 = bf16[3,512,2048]{2,1,0:T(8,128)(2,1)} fusion(f32[3,512,2048]{2,1,0:T(8,128)} %get-tuple-element.525, f32[3,512,2048]{2,1,0:T(8,128)S(1)} %bitcast.133, f32[3,512]{1,0:T(4,128)S(1)} %get-tuple-element.526), kind=kLoop, calls=%fused_computation.17.clone.1 | loop fusion | flops 9437184 | bytes 31463424 | tf_op jit(solution)/shard_map/while/body/eval_jaxpr/convert_element_type | solution.py:233
  544.9 5.8 fusion.147
  553.5 7.5 %fusion.148 = f32[2048,3,64]{0,2,1:T(8,128)} fusion(f32[3,512,2048]{2,1,0:T(8,128)} %get-tuple-element.525, f32[2048,3,64]{0,2,1:T(8,128)} %get-tuple-element.593, pred[]{:T(512)S(6)} %compare.4, bf16[2048,3,64]{0,2,1:T(8,128)(2,1)} %copy-done.17, s32[]{:T(128)S(6)} %select_n.304), kind=kOutput, calls=%fused_computation.27.clone.1 | convolution fusion | flops 406585344 | bytes 15925253 | tf_op jit(solution)/shard_map/while/body/eval_jaxpr/hqk,qhe->khe/dot_general | solution.py:222
  571.9 6.0 bitcast_convert_fusion
  593.9 21.7 %reduce-scatter.15.cloned.1.call-done = bf16[512,768]{1,0:T(8,128)(2,1)} async-done(((bf16[2048,768]{1,0:T(8,128)(2,1)}), bf16[512,768]{1,0:T(8,128)(2,1)}) %reduce-scatter.15.cloned.1.call-update) | async-done | bytes 786448 | tf_op jit(solution)/shard_map/reduce_scatter | solution.py:270
  634.7 59.4 %reduce-scatter.17.cloned.1.call-done = f32[480,128]{1,0:T(8,128)} async-done(((f32[3840,128]{1,0:T(8,128)}), f32[480,128]{1,0:T(8,128)}) %reduce-scatter.17.cloned.1.call-update) | async-done | bytes 245776 | tf_op jit(solution)/shard_map/reduce_scatter | solution.py:69
  (410 shorter events, 269.9 us)
Async XLA Ops:
  7.2 210.3 %copy-start = (bf16[768,768]{1,0:T(8,128)(2,1)S(1)}, bf16[768,768]{1,0:T(8,128)(2,1)}, u32[]{:S(2)}) copy-start(bf16[768,768]{1,0:T(8,128)(2,1)} %param.26) | copy-start | bytes 3538948
  7.2 13.6 %copy-start.55 = (f32[2,192]{1,0:T(2,128)S(1)}, f32[2,192]{1,0:T(2,128)}, u32[]{:S(2)}) copy-start(f32[2,192]{1,0:T(2,128)} %param.21) | copy-start | bytes 4612
  7.2 39.4 %all-gather.6.cloned.1.call-start = ((), (), s32[]{:S(2)}) async-start(), calls=%async_computation.6 | async-start | bytes 3932160 | tf_op jit(solution)/shard_map/all_gather | solution.py:100
  15.2 118.4 %all-gather.8.cloned.1.call-start = ((), (), s32[]{:S(2)}) async-start(), calls=%async_computation.7 | async-start | bytes 3932160 | tf_op jit(solution)/shard_map/all_gather | solution.py:146
  19.6 158.1 %reduce-scatter.7.cloned.1.call-start = ((), (), s32[]{:S(2)}) async-start(), calls=%async_computation.8 | async-start | bytes 3932160 | tf_op jit(solution)/shard_map/reduce_scatter | solution.py:153
  139.6 38.1 %copy-start.3 = (bf16[512,768]{1,0:T(8,128)(2,1)S(1)}, bf16[512,768]{1,0:T(8,128)(2,1)}, u32[]{:S(2)}) copy-start(bf16[512,768]{1,0:T(8,128)(2,1)} %param.16) | copy-start | bytes 2359300
  139.6 72.8 %all-gather.10.cloned.1.call-start = ((), (), s32[]{:S(2)}) async-start(), calls=%async_computation.9 | async-start | bytes 3932160 | tf_op jit(solution)/shard_map/all_gather | solution.py:161
  183.8 96.7 %reduce-scatter.9.cloned.1.call-start = ((), (), s32[]{:S(2)}) async-start(), calls=%async_computation.10 | async-start | bytes 3932160 | tf_op jit(solution)/shard_map/reduce_scatter | solution.py:176
  217.5 19.2 %copy-start.16 = (f32[2048,768]{1,0:T(8,128)}, f32[2048,768]{1,0:T(8,128)S(1)}, u32[]{:S(2)}) copy-start(f32[2048,768]{1,0:T(8,128)S(1)} %fusion.72) | copy-start | bytes 18874372
  217.5 20.9 %copy-start.60 = (bf16[768,768]{1,0:T(8,128)(2,1)S(1)}, bf16[768,768]{1,0:T(8,128)(2,1)}, u32[]{:S(2)}) copy-start(bf16[768,768]{1,0:T(8,128)(2,1)} %param.24) | copy-start | bytes 3538948
  242.5 79.5 %all-gather.12.cloned.1.call-start = ((), (), s32[]{:S(2)}) async-start(), calls=%async_computation.11 | async-start | bytes 3932160 | tf_op jit(solution)/shard_map/all_gather | solution.py:189
  289.9 271.1 %reduce-scatter.13.cloned.1.call-start = ((), (), s32[]{:S(2)}) async-start(), calls=%async_computation.13 | async-start | bytes 3932160 | tf_op jit(solution)/shard_map/reduce_scatter | solution.py:207
  332.9 231.0 %reduce-scatter.11.cloned.1.call-start = ((), (), s32[]{:S(2)}) async-start(), calls=%async_computation.12 | async-start | bytes 5971968 | tf_op jit(solution)/shard_map/reduce_scatter | solution.py:69
  338.7 277.0 %reduce-scatter.15.cloned.1.call-start = ((), (), s32[]{:S(2)}) async-start(), calls=%async_computation.14 | async-start | bytes 3932160 | tf_op jit(solution)/shard_map/reduce_scatter | solution.py:270
  339.7 221.3 %copy-start.4 = (bf16[512,768]{1,0:T(8,128)(2,1)S(1)}, bf16[512,768]{1,0:T(8,128)(2,1)}, u32[]{:S(2)}) copy-start(bf16[512,768]{1,0:T(8,128)(2,1)} %param.16) | copy-start | bytes 2359300
  339.7 221.3 %copy-start.26 = (f32[768]{0:T(1024)S(1)}, f32[768]{0:T(1024)}, u32[]{:S(2)}) copy-start(f32[768]{0:T(1024)} %get-tuple-element.286) | copy-start | bytes 9220
  339.7 221.3 %copy-start.30 = (f32[512]{0:T(512)S(1)}, f32[512]{0:T(512)}, u32[]{:S(2)}) copy-start(f32[512]{0:T(512)} %copy-done.27) | copy-start | bytes 6148
  339.7 221.3 %copy-start.44 = (f32[768]{0:T(1024)S(1)}, f32[768]{0:T(1024)}, u32[]{:S(2)}) copy-start(f32[768]{0:T(1024)} %get-tuple-element.285) | copy-start | bytes 9220
  356.9 12.7 %slice-start = ((s8[12582912]{0:T(1024)(128)(4,1)}), s8[4194304]{0:T(1024)(128)(4,1)S(1)}, s32[]{:S(2)}) async-start(s8[12582912]{0:T(1024)(128)(4,1)} %bitcast.132), calls=%async_computation.16 | async-start | bytes 8388608 | tf_op jit(solution)/shard_map/while
  356.9 12.7 %slice-start.1 = ((s8[12582912]{0:T(1024)(128)(4,1)}), s8[4194304]{0:T(1024)(128)(4,1)S(1)}, s32[]{:S(2)}) async-start(s8[12582912]{0:T(1024)(128)(4,1)} %bitcast.132), calls=%async_computation.17 | async-start | bytes 8388608 | tf_op jit(solution)/shard_map/while
  356.9 14.2 %slice-start.2 = ((s8[12582912]{0:T(1024)(128)(4,1)}), s8[4194304]{0:T(1024)(128)(4,1)S(1)}, s32[]{:S(2)}) async-start(s8[12582912]{0:T(1024)(128)(4,1)} %bitcast.132), calls=%async_computation.18 | async-start | bytes 8388608 | tf_op jit(solution)/shard_map/while
  411.8 14.3 %slice-start.2 = ((s8[12582912]{0:T(1024)(128)(4,1)}), s8[4194304]{0:T(1024)(128)(4,1)S(1)}, s32[]{:S(2)}) async-start(s8[12582912]{0:T(1024)(128)(4,1)} %bitcast.132), calls=%async_computation.18 | async-start | bytes 8388608 | tf_op jit(solution)/shard_map/while
  467.4 12.7 %slice-start = ((s8[12582912]{0:T(1024)(128)(4,1)}), s8[4194304]{0:T(1024)(128)(4,1)S(1)}, s32[]{:S(2)}) async-start(s8[12582912]{0:T(1024)(128)(4,1)} %bitcast.132), calls=%async_computation.16 | async-start | bytes 8388608 | tf_op jit(solution)/shard_map/while
  467.4 14.2 %slice-start.2 = ((s8[12582912]{0:T(1024)(128)(4,1)}), s8[4194304]{0:T(1024)(128)(4,1)S(1)}, s32[]{:S(2)}) async-start(s8[12582912]{0:T(1024)(128)(4,1)} %bitcast.132), calls=%async_computation.18 | async-start | bytes 8388608 | tf_op jit(solution)/shard_map/while
  522.5 14.0 %slice-start.2 = ((s8[12582912]{0:T(1024)(128)(4,1)}), s8[4194304]{0:T(1024)(128)(4,1)S(1)}, s32[]{:S(2)}) async-start(s8[12582912]{0:T(1024)(128)(4,1)} %bitcast.132), calls=%async_computation.18 | async-start | bytes 8388608 | tf_op jit(solution)/shard_map/while
  577.9 116.3 %reduce-scatter.17.cloned.1.call-start = ((), (), s32[]{:S(2)}) async-start(), calls=%async_computation.15 | async-start | bytes 2211840 | tf_op jit(solution)/shard_map/reduce_scatter | solution.py:69
  589.0 26.7 %copy-start.32 = (f32[768]{0:T(1024)S(1)}, f32[768]{0:T(1024)}, u32[]{:S(2)}) copy-start(f32[768]{0:T(1024)} %copy-done.31) | copy-start | bytes 9220
  589.0 26.7 %copy-start.34 = (f32[512]{0:T(512)S(1)}, f32[512]{0:T(512)}, u32[]{:S(2)}) copy-start(f32[512]{0:T(512)} %copy-done.33) | copy-start | bytes 6148
  589.0 28.4 %copy-start.42 = (f32[512]{0:T(512)S(1)}, f32[512]{0:T(512)}, u32[]{:S(2)}) copy-start(f32[512]{0:T(512)} %copy-done.41) | copy-start | bytes 6148
  589.0 28.5 %copy-start.38 = (f32[512]{0:T(512)S(1)}, f32[512]{0:T(512)}, u32[]{:S(2)}) copy-start(f32[512]{0:T(512)} %copy-done.37) | copy-start | bytes 6148
  589.0 31.2 %copy-start.54 = (f32[768]{0:T(1024)S(1)}, f32[768]{0:T(1024)}, u32[]{:S(2)}) copy-start(f32[768]{0:T(1024)} %get-tuple-element.341) | copy-start | bytes 9220
  631.0 74.5 %copy-start.1 = (bf16[768,768]{1,0:T(8,128)(2,1)S(1)}, bf16[768,768]{1,0:T(8,128)(2,1)}, u32[]{:S(2)}) copy-start(bf16[768,768]{1,0:T(8,128)(2,1)} %param.26) | copy-start | bytes 3538948
  (64 other events, 342.2 us)
Sparse Core Ops, SparseCore 0:
  15.3 31.2 all-gather.5
  48.7 28.4 all-gather.7
  139.8 37.8 reduce-scatter.6
  183.9 28.4 all-gather.9
  242.6 37.8 reduce-scatter.8
  290.0 28.5 all-gather.11
  333.0 37.9 reduce-scatter.12
  374.6 104.4 reduce-scatter.10
  578.0 37.6 reduce-scatter.14
  626.6 67.4 reduce-scatter.16

commit v3 on v2

--- a/solution.py
+++ b/solution.py
@@ -3,6 +3,8 @@
 import jax
 import jax.numpy as jnp
 from jax import lax
+from jax.experimental import pallas as pl
+from jax.experimental.pallas import tpu as pltpu
 from jax.sharding import PartitionSpec as P
 
 D = 768
@@ -12,7 +14,6 @@
 SIDE_S = 12
 SIDE_M = 15
 SIDE_L = 20
-BLOCK = 512
 TOK_DEV = 2048
 
 
@@ -60,6 +61,178 @@
     delta_row = row_query[:, None] - row_key[None, :]
     delta_col = col_query[:, None] - col_key[None, :]
     return jnp.sqrt(delta_row * delta_row + delta_col * delta_col)
+
+Q_BLOCK = 256
+K_BLOCK = 256
+NEG = -1e30
+
+
+def key_ranges(segment, tokens):
+    starts = jnp.arange(0, tokens, Q_BLOCK)
+    first = segment[starts]
+    last = segment[starts + Q_BLOCK - 1]
+    key_lo = jnp.sum(segment[None, :] < first[:, None], axis=1)
+    key_hi = jnp.sum(segment[None, :] <= last[:, None], axis=1)
+    return (key_lo // K_BLOCK).astype(jnp.int32), ((key_hi + K_BLOCK - 1) // K_BLOCK).astype(jnp.int32)
+
+
+def block_geometry(qi_ref, ki_ref, start):
+    rq = qi_ref[:, 0:1]
+    cq = qi_ref[:, 1:2]
+    sq = qi_ref[:, 2:3]
+    rk = ki_ref[0:1, pl.ds(start, K_BLOCK)]
+    ck = ki_ref[1:2, pl.ds(start, K_BLOCK)]
+    sk = ki_ref[2:3, pl.ds(start, K_BLOCK)]
+    dr = rq - rk
+    dc = cq - ck
+    return jnp.sqrt(dr * dr + dc * dc), sq == sk
+
+
+def fwd_kernel(heads, scale, lo_ref, hi_ref, slope_ref, q_ref, k_ref, v_ref, qi_ref, ki_ref, o_ref, lse_ref):
+    i = pl.program_id(0)
+    queries = [q_ref[h] for h in range(heads)]
+    width = q_ref.shape[2]
+
+    def body(kb, carry):
+        start = pl.multiple_of(kb * K_BLOCK, K_BLOCK)
+        dist, allowed = block_geometry(qi_ref, ki_ref, start)
+        out = []
+        for h in range(heads):
+            m_old, l_old, acc_old = carry[h]
+            keys = k_ref[h, pl.ds(start, K_BLOCK), :]
+            vals = v_ref[h, pl.ds(start, K_BLOCK), :]
+            s = lax.dot_general(queries[h], keys, (((1,), (1,)), ((), ())),
+                                preferred_element_type=jnp.float32) * scale - slope_ref[h] * dist
+            s = jnp.where(allowed, s, NEG)
+            m_new = jnp.maximum(m_old, jnp.max(s, axis=1, keepdims=True))
+            alpha = jnp.exp(m_old - m_new)
+            p = jnp.exp(s - m_new)
+            l_new = alpha * l_old + jnp.sum(p, axis=1, keepdims=True)
+            acc_new = alpha * acc_old + jnp.dot(p.astype(jnp.bfloat16), vals,
+                                                preferred_element_type=jnp.float32)
+            out.append((m_new, l_new, acc_new))
+        return tuple(out)
+
+    init = tuple(
+        (jnp.full((Q_BLOCK, 1), NEG, jnp.float32), jnp.zeros((Q_BLOCK, 1), jnp.float32),
+         jnp.zeros((Q_BLOCK, width), jnp.float32))
+        for _ in range(heads)
+    )
+    final = lax.fori_loop(lo_ref[i], hi_ref[i], body, init)
+    for h in range(heads):
+        m, l, acc = final[h]
+        o_ref[h] = acc / l
+        lse_ref[h] = m + jnp.log(l)
+
+
+def bwd_kernel(heads, scale, lo_ref, hi_ref, slope_ref, q_ref, k_ref, v_ref, qi_ref, ki_ref,
+               o_ref, do_ref, lse_ref, dq_ref, dk_ref, dv_ref):
+    i = pl.program_id(0)
+
+    @pl.when(i == 0)
+    def _():
+        dk_ref[...] = jnp.zeros_like(dk_ref)
+        dv_ref[...] = jnp.zeros_like(dv_ref)
+
+    queries = [q_ref[h] for h in range(heads)]
+    grads = [do_ref[h] for h in range(heads)]
+    lses = [lse_ref[h] for h in range(heads)]
+    deltas = [jnp.sum(grads[h].astype(jnp.float32) * o_ref[h], axis=1, keepdims=True)
+              for h in range(heads)]
+    width = q_ref.shape[2]
+
+    def body(kb, carry):
+        start = pl.multiple_of(kb * K_BLOCK, K_BLOCK)
+        dist, allowed = block_geometry(qi_ref, ki_ref, start)
+        out = []
+        for h in range(heads):
+            keys = k_ref[h, pl.ds(start, K_BLOCK), :]
+            vals = v_ref[h, pl.ds(start, K_BLOCK), :]
+            s = lax.dot_general(queries[h], keys, (((1,), (1,)), ((), ())),
+                                preferred_element_type=jnp.float32) * scale - slope_ref[h] * dist
+            p = jnp.where(allowed, jnp.exp(s - lses[h]), 0.0)
+            dp = lax.dot_general(grads[h], vals, (((1,), (1,)), ((), ())),
+                                 preferred_element_type=jnp.float32)
+            ds = (p * (dp - deltas[h])).astype(jnp.bfloat16)
+            out.append(carry[h] + jnp.dot(ds, keys, preferred_element_type=jnp.float32))
+            dk_ref[h, pl.ds(start, K_BLOCK), :] += lax.dot_general(
+                ds, queries[h], (((0,), (0,)), ((), ())), preferred_element_type=jnp.float32)
+            dv_ref[h, pl.ds(start, K_BLOCK), :] += lax.dot_general(
+                p.astype(jnp.bfloat16), grads[h], (((0,), (0,)), ((), ())),
+                preferred_element_type=jnp.float32)
+        return tuple(out)
+
+    init = tuple(jnp.zeros((Q_BLOCK, width), jnp.float32) for _ in range(heads))
+    final = lax.fori_loop(lo_ref[i], hi_ref[i], body, init)
+    for h in range(heads):
+        dq_ref[h] = final[h]
+
+
+def attention_fwd(lo, hi, slopes, q, k, v, qinfo, kinfo, scale):
+    heads, tokens, width = q.shape
+    grid = (tokens // Q_BLOCK,)
+    whole = lambda i, lo, hi: (0, 0, 0)
+    rows = lambda i, lo, hi: (0, i, 0)
+    return pl.pallas_call(
+        functools.partial(fwd_kernel, heads, scale),
+        grid_spec=pltpu.PrefetchScalarGridSpec(
+            num_scalar_prefetch=2,
+            grid=grid,
+            in_specs=[
+                pl.BlockSpec(memory_space=pltpu.SMEM),
+                pl.BlockSpec((heads, Q_BLOCK, width), rows),
+                pl.BlockSpec((heads, tokens, width), whole),
+                pl.BlockSpec((heads, tokens, width), whole),
+                pl.BlockSpec((Q_BLOCK, 3), lambda i, lo, hi: (i, 0)),
+                pl.BlockSpec((3, tokens), lambda i, lo, hi: (0, 0)),
+            ],
+            out_specs=[
+                pl.BlockSpec((heads, Q_BLOCK, width), rows),
+                pl.BlockSpec((heads, Q_BLOCK, 1), rows),
+            ],
+        ),
+        out_shape=[
+            jax.ShapeDtypeStruct((heads, tokens, width), jnp.float32),
+            jax.ShapeDtypeStruct((heads, tokens, 1), jnp.float32),
+        ],
+        compiler_params=pltpu.CompilerParams(dimension_semantics=("arbitrary",)),
+    )(lo, hi, slopes, q, k, v, qinfo, kinfo)
+
+
+def attention_bwd(lo, hi, slopes, q, k, v, qinfo, kinfo, o, do, lse, scale):
+    heads, tokens, width = q.shape
+    grid = (tokens // Q_BLOCK,)
+    whole = lambda i, lo, hi: (0, 0, 0)
+    rows = lambda i, lo, hi: (0, i, 0)
+    return pl.pallas_call(
+        functools.partial(bwd_kernel, heads, scale),
+        grid_spec=pltpu.PrefetchScalarGridSpec(
+            num_scalar_prefetch=2,
+            grid=grid,
+            in_specs=[
+                pl.BlockSpec(memory_space=pltpu.SMEM),
+                pl.BlockSpec((heads, Q_BLOCK, width), rows),
+                pl.BlockSpec((heads, tokens, width), whole),
+                pl.BlockSpec((heads, tokens, width), whole),
+                pl.BlockSpec((Q_BLOCK, 3), lambda i, lo, hi: (i, 0)),
+                pl.BlockSpec((3, tokens), lambda i, lo, hi: (0, 0)),
+                pl.BlockSpec((heads, Q_BLOCK, width), rows),
+                pl.BlockSpec((heads, Q_BLOCK, width), rows),
+                pl.BlockSpec((heads, Q_BLOCK, 1), rows),
+            ],
+            out_specs=[
+                pl.BlockSpec((heads, Q_BLOCK, width), rows),
+                pl.BlockSpec((heads, tokens, width), whole),
+                pl.BlockSpec((heads, tokens, width), whole),
+            ],
+        ),
+        out_shape=[
+            jax.ShapeDtypeStruct((heads, tokens, width), jnp.float32),
+            jax.ShapeDtypeStruct((heads, tokens, width), jnp.float32),
+            jax.ShapeDtypeStruct((heads, tokens, width), jnp.float32),
+        ],
+        compiler_params=pltpu.CompilerParams(dimension_semantics=("arbitrary",)),
+    )(lo, hi, slopes, q, k, v, qinfo, kinfo, o, do, lse)
 
 
 def scatter_rows(parts, dp_size):
@@ -91,7 +264,6 @@
     ff_here = w_up.shape[1]
     tensor_pos = lax.axis_index("tensor")
     score_scale = HEAD_DIM ** (-0.5)
-    block_count = TOK_DEV // BLOCK
     segment, grid_row, grid_col, is_valid = layout(counts[0])
     keep_rows = lax.dynamic_slice_in_dim(is_valid, tensor_pos * local_rows, local_rows)[:, None]
     slopes = slopes_of(tensor_pos * heads_here, heads_here)
@@ -100,56 +272,33 @@
     normed = lax.all_gather(normed_local, "tensor", axis=0, tiled=True)
     projected = jnp.einsum("td,dsc->tsc", normed, w_qkv, preferred_element_type=jnp.float32)
     queries = (projected[:, 0] + b_qv[0]).astype(jnp.bfloat16)
-    key_heads = projected[:, 1].astype(jnp.bfloat16).reshape(TOK_DEV, heads_here, HEAD_DIM)
-    value_heads = (
-        (projected[:, 2] + b_qv[1]).astype(jnp.bfloat16).reshape(TOK_DEV, heads_here, HEAD_DIM)
-    )
-
-    def block_scores(offset):
-        query_block = lax.dynamic_slice_in_dim(queries, offset, BLOCK).reshape(
-            BLOCK, heads_here, HEAD_DIM
-        )
-        raw_scores = (
-            jnp.einsum("qhe,khe->hqk", query_block, key_heads, preferred_element_type=jnp.float32)
-            * score_scale
-        )
-        near_dist = distances(
-            lax.dynamic_slice_in_dim(grid_row, offset, BLOCK),
-            lax.dynamic_slice_in_dim(grid_col, offset, BLOCK),
-            grid_row,
-            grid_col,
-        )
-        same_image = lax.dynamic_slice_in_dim(segment, offset, BLOCK)[:, None] == segment[None, :]
-        return (
-            query_block,
-            jnp.where(
-                same_image[None], raw_scores - slopes[:, None, None] * near_dist[None], -1e30
-            ),
-        )
-
-    def attend_block(block_index):
-        _, scores = block_scores(block_index * BLOCK)
-        highest_score = jnp.max(scores, axis=-1, keepdims=True)
-        exp_terms = jnp.exp(scores - highest_score)
-        totals = jnp.sum(exp_terms, axis=-1, keepdims=True)
-        weights = (exp_terms / totals).astype(jnp.bfloat16)
-        mixed_block = jnp.einsum(
-            "hqk,khe->qhe", weights, value_heads, preferred_element_type=jnp.float32
-        )
-        return (
-            mixed_block.reshape(BLOCK, width_here).astype(jnp.bfloat16),
-            highest_score[..., 0] + jnp.log(totals[..., 0]),
-        )
-
-    mixed_blocks, log_totals = lax.map(attend_block, jnp.arange(block_count, dtype=jnp.int32))
+    keys = projected[:, 1].astype(jnp.bfloat16)
+    values = (projected[:, 2] + b_qv[1]).astype(jnp.bfloat16)
+
+    def head_major(rows):
+        return rows.reshape(TOK_DEV, heads_here, HEAD_DIM).transpose(1, 0, 2)
+
+    def row_major(heads):
+        return heads.transpose(1, 0, 2).reshape(TOK_DEV, width_here)
+
+    key_lo, key_hi = key_ranges(segment, TOK_DEV)
+    segment_f = segment.astype(jnp.float32)
+    query_info = jnp.stack([grid_row, grid_col, segment_f], axis=1)
+    key_info = jnp.stack([grid_row, grid_col, segment_f], axis=0)
+    query_heads = head_major(queries)
+    key_heads = head_major(keys)
+    value_heads = head_major(values)
+    mixed_f32, log_totals = attention_fwd(
+        key_lo, key_hi, slopes, query_heads, key_heads, value_heads, query_info, key_info, score_scale
+    )
     upstream = cotangent.astype(jnp.float32)
     branch_grad = lax.all_gather(
         (keep_rows * upstream).astype(jnp.bfloat16), "tensor", axis=0, tiled=True
     )
-    mixed_blocks, log_totals, branch_grad = lax.optimization_barrier(
-        (mixed_blocks, log_totals, branch_grad)
-    )
-    mixed_rows = mixed_blocks.reshape(TOK_DEV, width_here)
+    mixed_f32, log_totals, branch_grad = lax.optimization_barrier(
+        (mixed_f32, log_totals, branch_grad)
+    )
+    mixed_rows = row_major(mixed_f32).astype(jnp.bfloat16)
     attended = lax.psum_scatter(
         jnp.dot(mixed_rows, w_out, preferred_element_type=jnp.float32).astype(jnp.bfloat16),
         "tensor",
@@ -209,54 +358,16 @@
     )
     result = (after_attn + keep_rows * (branch + out_bias[1])).astype(jnp.bfloat16)
     early_sum = scatter_rows(early_parts, dp_size)
-    mixed_heads = mixed_grad.reshape(TOK_DEV, heads_here, HEAD_DIM)
-
-    def back_block(running, block_index):
-        key_acc, value_acc = running
-        offset = block_index * BLOCK
-        query_block, scores = block_scores(offset)
-        weights = jnp.exp(
-            scores - lax.dynamic_index_in_dim(log_totals, block_index, keepdims=False)[..., None]
-        )
-        grad_block = lax.dynamic_slice_in_dim(mixed_heads, offset, BLOCK)
-        value_acc = value_acc + jnp.einsum(
-            "hqk,qhe->khe",
-            weights.astype(jnp.bfloat16),
-            grad_block,
-            preferred_element_type=jnp.float32,
-        )
-        weight_grad = jnp.einsum(
-            "qhe,khe->hqk", grad_block, value_heads, preferred_element_type=jnp.float32
-        )
-        score_grad = (
-            weights * (weight_grad - jnp.sum(weights * weight_grad, axis=-1, keepdims=True))
-        ).astype(jnp.bfloat16)
-        query_grad_block = (
-            jnp.einsum("hqk,khe->qhe", score_grad, key_heads, preferred_element_type=jnp.float32)
-            * score_scale
-        )
-        key_acc = (
-            key_acc
-            + jnp.einsum(
-                "hqk,qhe->khe", score_grad, query_block, preferred_element_type=jnp.float32
-            )
-            * score_scale
-        )
-        return (
-            (key_acc, value_acc),
-            query_grad_block.reshape(BLOCK, width_here).astype(jnp.bfloat16),
-        )
-
-    zero_heads = jnp.zeros((TOK_DEV, heads_here, HEAD_DIM), jnp.float32)
-    (key_acc, value_acc), query_blocks = lax.scan(
-        back_block, (zero_heads, zero_heads), jnp.arange(block_count, dtype=jnp.int32)
-    )
-    key_acc, value_acc, query_blocks, early_sum, result = lax.optimization_barrier(
-        (key_acc, value_acc, query_blocks, early_sum, result)
-    )
-    query_grad = query_blocks.reshape(TOK_DEV, width_here)
-    key_grad = key_acc.reshape(TOK_DEV, width_here).astype(jnp.bfloat16)
-    value_grad = value_acc.reshape(TOK_DEV, width_here).astype(jnp.bfloat16)
+    query_acc, key_acc, value_acc = attention_bwd(
+        key_lo, key_hi, slopes, query_heads, key_heads, value_heads, query_info, key_info,
+        mixed_f32, head_major(mixed_grad), log_totals, score_scale,
+    )
+    query_acc, key_acc, value_acc, early_sum, result = lax.optimization_barrier(
+        (query_acc, key_acc, value_acc, early_sum, result)
+    )
+    query_grad = row_major(query_acc * score_scale).astype(jnp.bfloat16)
+    key_grad = row_major(key_acc * score_scale).astype(jnp.bfloat16)
+    value_grad = row_major(value_acc).astype(jnp.bfloat16)
     projected_grad = jnp.stack([query_grad, key_grad, value_grad], axis=1)
     qv_bias_grad = jnp.stack(
         [

time: 718 us -> 626 us (0.87)
  matrix products: 237 us -> 67.8 us
  Pallas kernels: 0 us -> 94 us
  waiting for transfers between devices: 209 us -> 274 us
  other arithmetic: 134 us -> 71.6 us
  loops' own time: 14.3 us -> 0 us
  local copies, waits for them, and re-layouts: 94.7 us -> 86.8 us
    dot_general x28 -> x0, matrix products: 171 us -> none  [the longest x8 65.1 us: block_scores(): jnp.einsum('qhe,khe->hqk', query_block, key_heads, preferred_element_type...]
    pallas_call x0 -> x2, Pallas kernels: none -> 94 us  [the longest x1 52 us: attention_bwd(): pl.pallas_call(functools.partial(bwd_kernel, heads, scale), grid_spec=plt...]
    reduce_scatter x2, waiting for transfers between devices: 59.4 us -> 139 us  [scatter_rows(): summed = lax.psum_scatter(parts, 'dp', scatter_dimension=0, tiled=True)]
    convert_element_type x7 -> x4, other arithmetic: 33.9 us -> 9.58 us  [the longest x2 4.18 us: on_device(): segment_f = segment.astype(jnp.float32)]
    sqrt x8 -> x0, other arithmetic: 24.3 us -> none  [distances(): return jnp.sqrt(delta_row * delta_row + delta_col * delta_col)]
    dynamic_slice x40 -> x0, local copies, waits for them, and re-layouts: 18.8 us -> none  [the longest x8 7.64 us: on_device(): lax.map(attend_block, jnp.arange(block_count, dtype=jnp.int32))]
    reduce_sum x4 -> x1, other arithmetic: 17.9 us -> 0.22 us  [key_ranges(): key_hi = jnp.sum(segment[None, :] <= last[:, None], axis=1)]
    another operation x2 -> x0, loops' own time: 14.3 us -> none  [the longest x1 11.1 us: on_device(): lax.scan(back_block, (zero_heads, zero_heads), jnp.arange(block_count, dt...]
  transfers between devices with their start and end apart: 10 -> 10, of which waited for: 6 -> 7; matrix products, arithmetic and copies ran while one was open for 50% -> 18% of each run, Pallas kernels for 0% -> 15%
where the time goes in v3:
time: 626 us; the launch traced here: 617 us
  waiting for transfers between devices  274 us (44%)
  Pallas kernels  94 us (15%)
  local copies, waits for them, and re-layouts  86.8 us (14%)
  other arithmetic  71.6 us (11%)
  matrix products  67.8 us (11%)
  between operations  17.1 us (3%)
    reduce_scatter x2, waiting for transfers between devices, scatter_rows(): summed = lax.psum_scatter(parts, 'dp', scatter_dimension=0, tiled=True)  139 us
    pallas_call x1, Pallas kernels, attention_bwd(): pl.pallas_call(functools.partial(bwd_kernel, heads, scale), grid_spec=plt...  52 us
    pallas_call x1, Pallas kernels, attention_fwd(): pl.pallas_call(functools.partial(fwd_kernel, heads, scale), grid_spec=plt...  42 us
    reduce_scatter x1, waiting for transfers between devices, on_device(): lax.psum_scatter(jnp.dot(mixed_rows, w_out, preferred_element_type=jnp.fl...  37.9 us
    reduce_scatter x1, waiting for transfers between devices, on_device(): lax.psum_scatter(jnp.einsum('tf,df->td', pre_grad, w_up, preferred_elemen...  37.8 us
    all_gather x1, waiting for transfers between devices, on_device(): normed_two = lax.all_gather(normed_two_local, 'tensor', axis=0, tiled=True)  28.6 us
    dot_general x1, matrix products, on_device(): jnp.einsum('td,fd->tf', branch_grad, w_down, preferred_element_type=jnp.f...  20.2 us
    all_gather x1, waiting for transfers between devices, on_device(): normed = lax.all_gather(normed_local, 'tensor', axis=0, tiled=True)  15.5 us
  transfers between devices with their start and end apart: 10, of which 7 were waited for; matrix products, arithmetic and copies ran while one was open for 18% of the time, Pallas kernels for 15%

profile of v3, /device:TPU:0, one launch (start us, length us, event | category | flops | bytes accessed | tf_op | source)
XLA Modules:
  0.0 617.4 jit_solution(16235903887873134588)
XLA Ops:
  30.0 15.5 %all-gather.6.cloned.1.call-done = bf16[2048,768]{1,0:T(8,128)(2,1)} async-done(((bf16[512,768]{1,0:T(8,128)(2,1)}), bf16[2048,768]{1,0:T(8,128)(2,1)}) %all-gather.6.cloned.1.call-update) | async-done | bytes 3145744 | tf_op jit(solution)/shard_map/all_gather | solution.py:272
  45.5 4.1 fusion.52
  53.9 4.2 fusion.48
  58.1 3.3 copy.63
  61.4 3.3 copy.65
  64.7 3.4 fusion.23.q_ref
  69.6 42.0 %shard_map.203 = (f32[3,2048,64]{2,1,0:T(8,128)}, f32[3,2048,1]{2,1,0:T(8,128)}) custom-call(s32[8]{0:T(128)} %get-tuple-element.131.lo_ref, s32[8]{0:T(128)} %get-tuple-element.130.hi_ref, f32[3]{0:T(128)} %multiply_exponential_fusion.slope_ref, bf16[3,2048,64]{2,1,0:T(8,128)(2,1)} %fusion.23.q_ref, bf16[3,2048,64]{2,1,0:T(8,128)(2,1)} %bitcast.65, ...), custom_call_target="tpu_custom_call" | custom-call | tf_op jit(solution)/shard_map/pallas_call | solution.py:176
  111.5 3.2 convert_bitcast_fusion
  121.4 37.9 %reduce-scatter.7.cloned.1.call-done = bf16[512,768]{1,0:T(8,128)(2,1)} async-done(((bf16[2048,768]{1,0:T(8,128)(2,1)}), bf16[512,768]{1,0:T(8,128)(2,1)}) %reduce-scatter.7.cloned.1.call-update) | async-done | bytes 786448 | tf_op jit(solution)/shard_map/reduce_scatter | solution.py:302
  166.1 28.6 %all-gather.10.cloned.1.call-done = bf16[2048,768]{1,0:T(8,128)(2,1)} async-done(((bf16[512,768]{1,0:T(8,128)(2,1)}), bf16[2048,768]{1,0:T(8,128)(2,1)}) %all-gather.10.cloned.1.call-update) | async-done | bytes 3145744 | tf_op jit(solution)/shard_map/all_gather | solution.py:310
  194.7 5.0 fusion.53
  199.8 20.2 %convert_reduce_fusion = (f32[768]{0:T(1024)}, bf16[2048,768]{1,0:T(8,128)(2,1)S(1)}, f32[2048,768]{1,0:T(8,128)}) fusion(f32[2048,768]{1,0:T(8,128)S(1)} %fusion.53, f32[768]{0:T(1024)} %param.21, bf16[2048,768]{1,0:T(8,128)(2,1)S(1)} %copy-done.39, bf16[768,768]{1,0:T(8,128)(2,1)S(1)} %copy-done), kind=kOutput, calls=%fused_computation.5 | convolution fusion | flops 2533883136 | bytes 20060160 | tf_op jit(solution)/shard_map/td,fd->tf/dot_general | solution.py:320
  221.6 4.0 convolution_convert_fusion.1
  225.9 37.8 %reduce-scatter.9.cloned.1.call-done = bf16[512,768]{1,0:T(8,128)(2,1)} async-done(((bf16[2048,768]{1,0:T(8,128)(2,1)}), bf16[512,768]{1,0:T(8,128)(2,1)}) %reduce-scatter.9.cloned.1.call-update) | async-done | bytes 786448 | tf_op jit(solution)/shard_map/reduce_scatter | solution.py:325
  272.2 6.9 %fusion.55 = f32[768,768]{1,0:T(8,128)} fusion(bf16[2048,768]{1,0:T(8,128)(2,1)} %all-gather.10.cloned.1.call-done, bf16[2048,768]{1,0:T(8,128)(2,1)} %copy-done.43), kind=kOutput, calls=%fused_computation.187 | convolution fusion | flops 2415919104 | bytes 8650752 | tf_op jit(solution)/shard_map/td,tf->df/dot_general | solution.py:324
  279.1 3.8 reshape.667
  282.9 5.7 multiply_convert_fusion
  290.2 4.2 fusion.54
  294.4 3.5 reshape.666
  297.9 6.2 %convolution_convert_fusion = bf16[2048,768]{1,0:T(8,128)(2,1)} fusion(bf16[2048,768]{1,0:T(8,128)(2,1)} %copy-done.14, bf16[768,768]{1,0:T(8,128)(2,1)S(1)} %copy-done), kind=kOutput, calls=%fused_computation.22 | convolution fusion | flops 2417491968 | bytes 7471104 | tf_op jit(solution)/shard_map/dot_general | solution.py:313
  304.2 3.8 fusion.56
  309.4 6.7 %pad_maximum_fusion = f32[8,165888]{1,0:T(8,128)} fusion(f32[8,18432]{1,0:T(8,128)S(1)} %reshape.668, f32[8,73728]{1,0:T(8,128)} %reshape.667, f32[8,73728]{1,0:T(8,128)} %reshape.666), kind=kLoop, calls=%fused_computation.21 | loop fusion | flops 2654208 | bytes 10616832 | tf_op jit(solution)/shard_map/concatenate | solution.py:345
  317.4 5.6 reshape.670
  324.7 52.0 %shard_map.204 = (f32[3,2048,64]{2,1,0:T(8,128)}, f32[3,2048,64]{2,1,0:T(8,128)}, f32[3,2048,64]{2,1,0:T(8,128)}) custom-call(s32[8]{0:T(128)} %get-tuple-element.131.lo_ref, s32[8]{0:T(128)} %get-tuple-element.130.hi_ref, f32[3]{0:T(128)} %multiply_exponential_fusion.slope_ref, bf16[3,2048,64]{2,1,0:T(8,128)(2,1)} %fusion.23.q_ref, ...), custom_call_target="tpu_custom_call" | custom-call | tf_op jit(solution)/shard_map/pallas_call | solution.py:207
  379.2 84.7 %reduce-scatter.11.cloned.1.call-done = f32[1296,128]{1,0:T(8,128)} async-done(((f32[10368,128]{1,0:T(8,128)}), f32[1296,128]{1,0:T(8,128)}) %reduce-scatter.11.cloned.1.call-update) | async-done | bytes 663568 | tf_op jit(solution)/shard_map/reduce_scatter | solution.py:242
  476.0 6.2 %bitcast_convert_fusion = bf16[2048,768]{1,0:T(8,128)(2,1)} fusion(bf16[768,3,192]{0,2,1:T(8,128)(2,1)} %param.16, bf16[2048,1,192]{0,2,1:T(8,128)(2,1)} %bitcast.78, bf16[2048,1,192]{0,2,1:T(8,128)(2,1)} %bitcast.74, bf16[2048,1,192]{0,2,1:T(8,128)(2,1)} %bitcast.76), kind=kOutput, calls=%fused_computation.4 | convolution fusion | flops 1815871488 | bytes 6389760 | tf_op jit(solution)/shard_map/tsc,dsc->td/dot_general | solution.py:382
  492.2 3.2 fusion.57
  495.4 4.2 copy.74
  499.7 5.1 reshape.672
  504.8 15.2 %reduce-scatter.15.cloned.1.call-done = bf16[512,768]{1,0:T(8,128)(2,1)} async-done(((bf16[2048,768]{1,0:T(8,128)(2,1)}), bf16[512,768]{1,0:T(8,128)(2,1)}) %reduce-scatter.15.cloned.1.call-update) | async-done | bytes 786448 | tf_op jit(solution)/shard_map/reduce_scatter | solution.py:381
  544.8 54.0 %reduce-scatter.17.cloned.1.call-done = f32[480,128]{1,0:T(8,128)} async-done(((f32[3840,128]{1,0:T(8,128)}), f32[480,128]{1,0:T(8,128)}) %reduce-scatter.17.cloned.1.call-update) | async-done | bytes 245776 | tf_op jit(solution)/shard_map/reduce_scatter | solution.py:242
  599.6 5.3 all-gather
  (222 shorter events, 111.2 us)
Async XLA Ops:
  7.2 192.6 %copy-start = (bf16[768,768]{1,0:T(8,128)(2,1)S(1)}, bf16[768,768]{1,0:T(8,128)(2,1)}, u32[]{:S(2)}) copy-start(bf16[768,768]{1,0:T(8,128)(2,1)} %param.22) | copy-start | bytes 3538948
  7.2 6.9 %copy-start.34 = (s32[1,3]{1,0:T(1,128)S(1)}, s32[1,3]{1,0:T(1,128)}, u32[]{:S(2)}) copy-start(s32[1,3]{1,0:T(1,128)} %param.13) | copy-start | bytes 40
  7.2 9.6 %copy-start.6 = (bf16[512,768]{1,0:T(8,128)(2,1)S(1)}, bf16[512,768]{1,0:T(8,128)(2,1)}, u32[]{:S(2)}) copy-start(bf16[512,768]{1,0:T(8,128)(2,1)} %param.23) | copy-start | bytes 2359300
  7.2 38.3 %all-gather.6.cloned.1.call-start = ((), (), s32[]{:S(2)}) async-start(), calls=%async_computation.6 | async-start | bytes 3932160 | tf_op jit(solution)/shard_map/all_gather | solution.py:272
  10.2 7.6 %copy-start.18 = (f32[512]{0:T(512)}, f32[512]{0:T(512)S(1)}, u32[]{:S(2)}) copy-start(f32[512]{0:T(512)S(1)} %fusion.41) | copy-start | bytes 6148
  14.0 97.5 %all-gather.8.cloned.1.call-start = ((), (), s32[]{:S(2)}) async-start(), calls=%async_computation.7 | async-start | bytes 3932160 | tf_op jit(solution)/shard_map/all_gather | solution.py:295
  17.9 141.5 %reduce-scatter.7.cloned.1.call-start = ((), (), s32[]{:S(2)}) async-start(), calls=%async_computation.8 | async-start | bytes 3932160 | tf_op jit(solution)/shard_map/reduce_scatter | solution.py:302
  120.1 39.2 %copy-start.1 = (bf16[512,768]{1,0:T(8,128)(2,1)S(1)}, bf16[512,768]{1,0:T(8,128)(2,1)}, u32[]{:S(2)}) copy-start(bf16[512,768]{1,0:T(8,128)(2,1)} %param.12) | copy-start | bytes 2359300
  120.1 74.6 %all-gather.10.cloned.1.call-start = ((), (), s32[]{:S(2)}) async-start(), calls=%async_computation.9 | async-start | bytes 3932160 | tf_op jit(solution)/shard_map/all_gather | solution.py:310
  166.1 97.6 %reduce-scatter.9.cloned.1.call-start = ((), (), s32[]{:S(2)}) async-start(), calls=%async_computation.10 | async-start | bytes 3932160 | tf_op jit(solution)/shard_map/reduce_scatter | solution.py:325
  199.8 20.2 %copy-start.9 = (f32[2048,768]{1,0:T(8,128)}, f32[2048,768]{1,0:T(8,128)S(1)}, u32[]{:S(2)}) copy-start(f32[2048,768]{1,0:T(8,128)S(1)} %fusion.53) | copy-start | bytes 18874372
  199.8 21.8 %copy-start.42 = (bf16[768,768]{1,0:T(8,128)(2,1)S(1)}, bf16[768,768]{1,0:T(8,128)(2,1)}, u32[]{:S(2)}) copy-start(bf16[768,768]{1,0:T(8,128)(2,1)} %param.20) | copy-start | bytes 3538948
  225.7 78.5 %all-gather.12.cloned.1.call-start = ((), (), s32[]{:S(2)}) async-start(), calls=%async_computation.11 | async-start | bytes 3932160 | tf_op jit(solution)/shard_map/all_gather | solution.py:338
  272.1 104.5 %reduce-scatter.13.cloned.1.call-start = ((), (), s32[]{:S(2)}) async-start(), calls=%async_computation.13 | async-start | bytes 3932160 | tf_op jit(solution)/shard_map/reduce_scatter | solution.py:356
  282.9 7.4 %copy-start.40 = (bf16[2048,768]{1,0:T(8,128)(2,1)S(1)}, bf16[2048,768]{1,0:T(8,128)(2,1)}, u32[]{:S(2)}) copy-start(bf16[2048,768]{1,0:T(8,128)(2,1)} %all-gather.8.cloned.1.call-done) | copy-start | bytes 9437188
  309.4 6.8 %copy-start.16 = (bf16[192,768]{1,0:T(8,128)(2,1)S(1)}, bf16[192,768]{1,0:T(8,128)(2,1)}, u32[]{:S(2)}) copy-start(bf16[192,768]{1,0:T(8,128)(2,1)} %param.18) | copy-start | bytes 884740
  309.4 6.8 %copy-start.41 = (bf16[2048,768]{1,0:T(8,128)(2,1)S(1)}, bf16[2048,768]{1,0:T(8,128)(2,1)}, u32[]{:S(2)}) copy-start(bf16[2048,768]{1,0:T(8,128)(2,1)} %all-gather.12.cloned.1.call-done) | copy-start | bytes 9437188
  317.4 146.6 %reduce-scatter.11.cloned.1.call-start = ((), (), s32[]{:S(2)}) async-start(), calls=%async_computation.12 | async-start | bytes 5971968 | tf_op jit(solution)/shard_map/reduce_scatter | solution.py:242
  323.0 196.9 %reduce-scatter.15.cloned.1.call-start = ((), (), s32[]{:S(2)}) async-start(), calls=%async_computation.14 | async-start | bytes 3932160 | tf_op jit(solution)/shard_map/reduce_scatter | solution.py:381
  324.7 52.0 %copy-start.27 = (f32[768]{0:T(1024)S(1)}, f32[768]{0:T(1024)}, u32[]{:S(2)}) copy-start(f32[768]{0:T(1024)} %get-tuple-element.98) | copy-start | bytes 9220
  482.2 7.3 %copy-start.11 = (bf16[2048,3,64]{0,2,1:T(8,128)(2,1)S(1)}, bf16[2048,3,64]{0,2,1:T(8,128)(2,1)}, u32[]{:S(2)}) copy-start(bf16[2048,3,64]{0,2,1:T(8,128)(2,1)} %copy.72) | copy-start | bytes 2359300
  482.2 7.3 %copy-start.12 = (bf16[2048,3,64]{0,2,1:T(8,128)(2,1)S(1)}, bf16[2048,3,64]{0,2,1:T(8,128)(2,1)}, u32[]{:S(2)}) copy-start(bf16[2048,3,64]{0,2,1:T(8,128)(2,1)} %copy.71) | copy-start | bytes 2359300
  482.3 116.5 %reduce-scatter.17.cloned.1.call-start = ((), (), s32[]{:S(2)}) async-start(), calls=%async_computation.15 | async-start | bytes 2211840 | tf_op jit(solution)/shard_map/reduce_scatter | solution.py:242
  499.7 22.0 %copy-start.25 = (f32[512]{0:T(512)S(1)}, f32[512]{0:T(512)}, u32[]{:S(2)}) copy-start(f32[512]{0:T(512)} %copy-done.24) | copy-start | bytes 6148
  499.7 22.0 %copy-start.31 = (f32[1,768]{1,0:T(1,128)S(1)}, f32[1,768]{1,0:T(1,128)}, u32[]{:S(2)}) copy-start(f32[1,768]{1,0:T(1,128)} %reshape.677) | copy-start | bytes 9220
  499.7 22.1 %copy-start.19 = (f32[512]{0:T(512)S(1)}, f32[512]{0:T(512)}, u32[]{:S(2)}) copy-start(f32[512]{0:T(512)} %copy-done.18) | copy-start | bytes 6148
  504.7 19.7 %copy-start.30 = (f32[1,768]{1,0:T(1,128)S(1)}, f32[1,768]{1,0:T(1,128)}, u32[]{:S(2)}) copy-start(f32[1,768]{1,0:T(1,128)} %reshape.674) | copy-start | bytes 9220
  504.7 19.7 %copy-start.22 = (f32[5760]{0:T(1024)S(1)}, f32[5760]{0:T(1024)}, u32[]{:S(2)}) copy-start(f32[5760]{0:T(1024)} %custom-call) | copy-start | bytes 69124
  504.7 19.8 %copy-start.21 = (f32[1536]{0:T(1024)S(1)}, f32[1536]{0:T(1024)}, u32[]{:S(2)}) copy-start(f32[1536]{0:T(1024)} %reshape.679) | copy-start | bytes 18436
  504.7 19.8 %copy-start.32 = (f32[384]{0:T(512)S(1)}, f32[384]{0:T(512)}, u32[]{:S(2)}) copy-start(f32[384]{0:T(512)} %reshape.680) | copy-start | bytes 4612
  504.7 19.8 %copy-start.36 = (f32[768]{0:T(1024)S(1)}, f32[768]{0:T(1024)}, u32[]{:S(2)}) copy-start(f32[768]{0:T(1024)} %get-tuple-element.106) | copy-start | bytes 9220
  530.9 11.0 %copy-start.4 = (f32[512,768]{1,0:T(8,128)S(1)}, f32[512,768]{1,0:T(8,128)}, u32[]{:S(2)}) copy-start(f32[512,768]{1,0:T(8,128)} %copy-done.3) | copy-start | bytes 4718596
  (22 other events, 61.4 us)
Sparse Core Ops, SparseCore 0:
  14.2 31.2 all-gather.5
  47.6 28.4 all-gather.7
  120.3 39.0 reduce-scatter.6
  166.2 28.4 all-gather.9
  225.8 37.8 reduce-scatter.8
  272.3 28.4 all-gather.11
  317.5 37.9 reduce-scatter.12
  359.1 104.8 reduce-scatter.10
  482.4 37.5 reduce-scatter.14
  531.0 67.7 reduce-scatter.16

commit v4 on v3

--- a/solution.py
+++ b/solution.py
@@ -268,8 +268,8 @@
     keep_rows = lax.dynamic_slice_in_dim(is_valid, tensor_pos * local_rows, local_rows)[:, None]
     slopes = slopes_of(tensor_pos * heads_here, heads_here)
     inputs = patches.astype(jnp.float32)
-    normed_local = normalize(inputs, norm_gain[0], norm_bias[0]).astype(jnp.bfloat16)
-    normed = lax.all_gather(normed_local, "tensor", axis=0, tiled=True)
+    inputs_all = lax.all_gather(patches, "tensor", axis=0, tiled=True).astype(jnp.float32)
+    normed = normalize(inputs_all, norm_gain[0], norm_bias[0]).astype(jnp.bfloat16)
     projected = jnp.einsum("td,dsc->tsc", normed, w_qkv, preferred_element_type=jnp.float32)
     queries = (projected[:, 0] + b_qv[0]).astype(jnp.bfloat16)
     keys = projected[:, 1].astype(jnp.bfloat16)
@@ -299,15 +299,12 @@
         (mixed_f32, log_totals, branch_grad)
     )
     mixed_rows = row_major(mixed_f32).astype(jnp.bfloat16)
-    attended = lax.psum_scatter(
-        jnp.dot(mixed_rows, w_out, preferred_element_type=jnp.float32).astype(jnp.bfloat16),
-        "tensor",
-        scatter_dimension=0,
-        tiled=True,
-    ).astype(jnp.float32)
-    after_attn = inputs + keep_rows * (attended + out_bias[0])
-    normed_two_local = normalize(after_attn, norm_gain[1], norm_bias[1]).astype(jnp.bfloat16)
-    normed_two = lax.all_gather(normed_two_local, "tensor", axis=0, tiled=True)
+    mixed_all = lax.all_gather(mixed_rows, "tensor", axis=1, tiled=True)
+    w_out_all = lax.all_gather(w_out, "tensor", axis=0, tiled=True)
+    attended = jnp.dot(mixed_all, w_out_all, preferred_element_type=jnp.float32)
+    after_attn_all = inputs_all + is_valid[:, None] * (attended + out_bias[0])
+    after_attn = lax.dynamic_slice_in_dim(after_attn_all, tensor_pos * local_rows, local_rows)
+    normed_two = normalize(after_attn_all, norm_gain[1], norm_bias[1]).astype(jnp.bfloat16)
     hidden_pre = jnp.dot(normed_two, w_up, preferred_element_type=jnp.float32) + b_up
     hidden = jax.nn.gelu(hidden_pre, approximate=False).astype(jnp.bfloat16)
     branch_partial = jnp.dot(hidden, w_down, preferred_element_type=jnp.float32).astype(

time: 626 us -> 601 us (0.960)
  waiting for transfers between devices: 274 us -> 239 us
  local copies, waits for them, and re-layouts: 86.8 us -> 106 us
  Pallas kernels: 94 us -> 75.8 us
  other arithmetic: 71.6 us -> 79.2 us
    reduce_scatter x1 -> x0, waiting for transfers between devices: 37.9 us -> none  [on_device(): lax.psum_scatter(jnp.dot(mixed_rows, w_out, preferred_element_type=jnp.fl...]
    unnamed x96 -> x84, local copies, waits for them, and re-layouts: 13.1 us -> 25 us
    pallas_call x1, Pallas kernels: 52 us -> 42 us  [attention_bwd(): pl.pallas_call(functools.partial(bwd_kernel, heads, scale), grid_spec=plt...]
    pallas_call x1, Pallas kernels: 42 us -> 33.8 us  [attention_fwd(): pl.pallas_call(functools.partial(fwd_kernel, heads, scale), grid_spec=plt...]
    all_gather x2 -> x3, waiting for transfers between devices: 44.1 us -> 50.2 us  [the longest x1 36.3 us: on_device(): mixed_all = lax.all_gather(mixed_rows, 'tensor', axis=1, tiled=True)]
  transfers between devices with their start and end apart: 10 -> 10, of which waited for: 7 -> 6; matrix products, arithmetic and copies ran while one was open for 18% -> 22% of each run, Pallas kernels for 15% -> 13%
where the time goes in v4:
time: 601 us; the launch traced here: 589 us
  waiting for transfers between devices  239 us (40%)
  local copies, waits for them, and re-layouts  106 us (18%)
  other arithmetic  79.2 us (13%)
  Pallas kernels  75.8 us (13%)
  matrix products  67.5 us (11%)
  between operations  16.8 us (3%)
    reduce_scatter x2, waiting for transfers between devices, scatter_rows(): summed = lax.psum_scatter(parts, 'dp', scatter_dimension=0, tiled=True)  142 us
    pallas_call x1, Pallas kernels, attention_bwd(): pl.pallas_call(functools.partial(bwd_kernel, heads, scale), grid_spec=plt...  42 us
    all_gather x1, waiting for transfers between devices, on_device(): mixed_all = lax.all_gather(mixed_rows, 'tensor', axis=1, tiled=True)  36.3 us
    reduce_scatter x1, waiting for transfers between devices, on_device(): lax.psum_scatter(jnp.einsum('tf,df->td', pre_grad, w_up, preferred_elemen...  36.2 us
    pallas_call x1, Pallas kernels, attention_fwd(): pl.pallas_call(functools.partial(fwd_kernel, heads, scale), grid_spec=plt...  33.8 us
    unnamed x84, local copies, waits for them, and re-layouts  25 us
    dot_general x1, matrix products, on_device(): jnp.einsum('td,fd->tf', branch_grad, w_down, preferred_element_type=jnp.f...  19.9 us
    all_gather x1, waiting for transfers between devices, on_device(): lax.all_gather(patches, 'tensor', axis=0, tiled=True).astype(jnp.float32)  13.8 us
  transfers between devices with their start and end apart: 10, of which 6 were waited for; matrix products, arithmetic and copies ran while one was open for 22% of the time, Pallas kernels for 13%

profile of v4, /device:TPU:0, one launch (start us, length us, event | category | flops | bytes accessed | tf_op | source)
XLA Modules:
  0.0 589.4 jit_solution(13961433465138582257)
XLA Ops:
  27.7 13.8 %all-gather.7.cloned.1.call-done = bf16[2048,768]{0,1:T(8,128)(2,1)} async-done(((bf16[512,768]{0,1:T(8,128)(2,1)}), bf16[2048,768]{0,1:T(8,128)(2,1)}) %all-gather.7.cloned.1.call-update) | async-done | bytes 3145744 | tf_op jit(solution)/shard_map/all_gather | solution.py:271
  51.3 3.4 copy.105
  54.6 3.4 copy.107
  58.0 3.5 fusion.26.q_ref
  62.9 33.8 %shard_map.203 = (f32[3,2048,64]{2,1,0:T(8,128)}, f32[3,2048,1]{2,1,0:T(8,128)}) custom-call(s32[8]{0:T(128)} %get-tuple-element.148.lo_ref, s32[8]{0:T(128)} %get-tuple-element.147.hi_ref, f32[3]{0:T(128)} %multiply_exponential_fusion.slope_ref, bf16[3,2048,64]{2,1,0:T(8,128)(2,1)} %fusion.26.q_ref, bf16[3,2048,64]{2,1,0:T(8,128)(2,1)} %bitcast.63, ...), custom_call_target="tpu_custom_call" | custom-call | tf_op jit(solution)/shard_map/pallas_call | solution.py:176
  103.1 36.3 %all-gather.11.cloned.1.call-done = bf16[2048,768]{0,1:T(8,128)(2,1)} async-done(((bf16[2048,192]{0,1:T(8,128)(2,1)}), bf16[2048,768]{0,1:T(8,128)(2,1)}) %all-gather.11.cloned.1.call-update) | async-done | bytes 3145744 | tf_op jit(solution)/shard_map/all_gather | solution.py:302
  139.4 6.7 %fusion.59 = (f32[2048]{0:T(1024)S(1)}, f32[2048,768]{0,1:T(8,128)S(1)}) fusion(f32[768]{0:T(1024)S(1)} %get-tuple-element.112, bf16[2048,768]{0,1:T(8,128)(2,1)} %all-gather.11.cloned.1.call-done, bf16[768,768]{1,0:T(8,128)(2,1)} %all-gather.13.cloned.1.call-done, f32[2048]{0:T(1024)S(1)} %fusion.39, bf16[2048,768]{0,1:T(8,128)(2,1)} %all-gather.7.cloned.1.call-done), kind=kOutput, calls=%fused_computation.196 | convolution fusion | flops 2423781376 | bytes 13782016 | tf_op jit(solution)/shard_map/dot_general | solution.py:304
  153.1 19.9 %convert_reduce_fusion.1 = (f32[768]{0:T(1024)}, bf16[2048,768]{1,0:T(8,128)(2,1)S(1)}, f32[2048,768]{1,0:T(8,128)}) fusion(f32[2048,768]{1,0:T(8,128)S(1)} %fusion.60, f32[768]{0:T(1024)S(1)} %copy-done.28, bf16[2048,768]{0,1:T(8,128)(2,1)S(1)} %copy-done.31, bf16[768,768]{1,0:T(8,128)(2,1)S(1)} %copy-done), kind=kOutput, calls=%fused_computation.14 | convolution fusion | flops 2533883136 | bytes 20060160 | tf_op jit(solution)/shard_map/td,fd->tf/dot_general | solution.py:317
  174.6 4.0 convolution_convert_fusion.1
  180.3 36.2 %reduce-scatter.6.cloned.1.call-done = bf16[512,768]{0,1:T(8,128)(2,1)} async-done(((bf16[2048,768]{0,1:T(8,128)(2,1)}), bf16[512,768]{0,1:T(8,128)(2,1)}) %reduce-scatter.6.cloned.1.call-update) | async-done | bytes 786448 | tf_op jit(solution)/shard_map/reduce_scatter | solution.py:322
  222.1 4.1 multiply_reduce_fusion.2
  226.3 6.9 %fusion.62 = f32[768,768]{1,0:T(8,128)} fusion(bf16[2048,768]{0,1:T(8,128)(2,1)} %copy-done.11, bf16[2048,768]{1,0:T(8,128)(2,1)} %copy-done.35), kind=kOutput, calls=%fused_computation.199 | convolution fusion | flops 2415919104 | bytes 8650752 | tf_op jit(solution)/shard_map/td,tf->df/dot_general | solution.py:321
  233.2 3.6 reshape.694
  236.8 5.7 multiply_convert_fusion
  244.2 4.1 fusion.61
  248.4 3.5 reshape.693
  251.8 6.2 %convolution_convert_fusion = bf16[2048,768]{0,1:T(8,128)(2,1)} fusion(bf16[2048,768]{1,0:T(8,128)(2,1)} %copy-done.12, bf16[768,768]{1,0:T(8,128)(2,1)S(1)} %copy-done), kind=kOutput, calls=%fused_computation.33 | convolution fusion | flops 2417491968 | bytes 7471104 | tf_op jit(solution)/shard_map/dot_general | solution.py:310
  258.1 3.8 fusion.63
  263.3 6.5 %pad_maximum_fusion = f32[8,165888]{1,0:T(8,128)} fusion(f32[8,18432]{1,0:T(8,128)S(1)} %reshape.695, f32[8,73728]{1,0:T(8,128)} %reshape.694, f32[8,73728]{1,0:T(8,128)} %reshape.693), kind=kLoop, calls=%fused_computation.32 | loop fusion | flops 2654208 | bytes 10616832 | tf_op jit(solution)/shard_map/concatenate | solution.py:342
  270.6 5.7 reshape.697
  277.9 42.0 %shard_map.204 = (f32[3,2048,64]{2,1,0:T(8,128)}, f32[3,2048,64]{2,1,0:T(8,128)}, f32[3,2048,64]{2,1,0:T(8,128)}) custom-call(s32[8]{0:T(128)} %get-tuple-element.148.lo_ref, s32[8]{0:T(128)} %get-tuple-element.147.hi_ref, f32[3]{0:T(128)} %multiply_exponential_fusion.slope_ref, bf16[3,2048,64]{2,1,0:T(8,128)(2,1)} %fusion.26.q_ref, ...), custom_call_target="tpu_custom_call" | custom-call | tf_op jit(solution)/shard_map/pallas_call | solution.py:207
  322.8 93.8 %reduce-scatter.8.cloned.1.call-done = f32[1296,128]{1,0:T(8,128)} async-done(((f32[10368,128]{1,0:T(8,128)}), f32[1296,128]{1,0:T(8,128)}) %reduce-scatter.8.cloned.1.call-update) | async-done | bytes 663568 | tf_op jit(solution)/shard_map/reduce_scatter | solution.py:242
  421.6 4.3 convert_reduce_fusion.3
  428.4 3.9 convert_reduce_fusion.2
  434.7 6.0 %bitcast_convert_fusion = bf16[2048,768]{0,1:T(8,128)(2,1)} fusion(bf16[768,3,192]{0,2,1:T(8,128)(2,1)} %param.16, bf16[2048,1,192]{0,2,1:T(8,128)(2,1)} %bitcast.74, bf16[2048,1,192]{0,2,1:T(8,128)(2,1)S(1)} %bitcast.70, bf16[2048,1,192]{0,2,1:T(8,128)(2,1)} %bitcast.72), kind=kOutput, calls=%fused_computation.13 | convolution fusion | flops 1815871488 | bytes 6389760 | tf_op jit(solution)/shard_map/tsc,dsc->td/dot_general | solution.py:379
  455.7 4.2 fusion.49
  459.9 4.4 copy.122
  464.3 5.0 reshape.699
  469.3 9.0 %reduce-scatter.12.cloned.1.call-done = bf16[512,768]{0,1:T(8,128)(2,1)} async-done(((bf16[2048,768]{0,1:T(8,128)(2,1)}), bf16[512,768]{0,1:T(8,128)(2,1)}) %reduce-scatter.12.cloned.1.call-update) | async-done | bytes 786448 | tf_op jit(solution)/shard_map/reduce_scatter | solution.py:378
  516.4 3.7 add_convert_fusion.4
  522.4 48.6 %reduce-scatter.14.cloned.1.call-done = f32[480,128]{1,0:T(8,128)} async-done(((f32[3840,128]{1,0:T(8,128)}), f32[480,128]{1,0:T(8,128)}) %reduce-scatter.14.cloned.1.call-update) | async-done | bytes 245776 | tf_op jit(solution)/shard_map/reduce_scatter | solution.py:242
  571.8 5.3 all-gather
  (212 shorter events, 131.4 us)
Async XLA Ops:
  7.2 145.6 %copy-start = (bf16[768,768]{1,0:T(8,128)(2,1)S(1)}, bf16[768,768]{1,0:T(8,128)(2,1)}, u32[]{:S(2)}) copy-start(bf16[768,768]{1,0:T(8,128)(2,1)} %param.22) | copy-start | bytes 3538948
  7.2 4.0 copy-start.27
  7.2 16.1 %copy-start.30 = (f32[2,192]{1,0:T(2,128)S(1)}, f32[2,192]{1,0:T(2,128)}, u32[]{:S(2)}) copy-start(f32[2,192]{1,0:T(2,128)} %param.17) | copy-start | bytes 4612
  7.2 34.3 %all-gather.7.cloned.1.call-start = ((), (), s32[]{:S(2)}) async-start(), calls=%async_computation.5 | async-start | bytes 3932160 | tf_op jit(solution)/shard_map/all_gather | solution.py:271
  9.7 87.0 %all-gather.9.cloned.1.call-start = ((), (), s32[]{:S(2)}) async-start(), calls=%async_computation.6 | async-start | bytes 3932160 | tf_op jit(solution)/shard_map/all_gather | solution.py:295
  9.7 17.3 %copy-start.24 = (f32[2,768]{1,0:T(2,128)S(1)}, f32[2,768]{1,0:T(2,128)}, u32[]{:S(2)}) copy-start(f32[2,768]{1,0:T(2,128)} %param.15) | copy-start | bytes 18436
  9.7 17.3 %copy-start.25 = (f32[2,768]{1,0:T(2,128)S(1)}, f32[2,768]{1,0:T(2,128)}, u32[]{:S(2)}) copy-start(f32[2,768]{1,0:T(2,128)} %param.14) | copy-start | bytes 18436
  14.9 88.2 %all-gather.13.cloned.1.call-start = ((), (), s32[]{:S(2)}) async-start(), calls=%async_computation.8 | async-start | bytes 1474560 | tf_op jit(solution)/shard_map/all_gather | solution.py:303
  15.6 123.8 %all-gather.11.cloned.1.call-start = ((), (), s32[]{:S(2)}) async-start(), calls=%async_computation.7 | async-start | bytes 3932160 | tf_op jit(solution)/shard_map/all_gather | solution.py:302
  27.1 18.2 %copy-start.29 = (f32[768]{0:T(1024)}, f32[768]{0:T(1024)S(1)}, u32[]{:S(2)}) copy-start(f32[768]{0:T(1024)S(1)} %get-tuple-element.116) | copy-start | bytes 9220
  41.5 3.7 copy-start.34
  44.3 3.1 copy-start.14
  58.0 3.5 copy-start.5
  96.7 5.8 copy-start.26
  102.4 114.1 %reduce-scatter.6.cloned.1.call-start = ((), (), s32[]{:S(2)}) async-start(), calls=%async_computation.9 | async-start | bytes 3932160 | tf_op jit(solution)/shard_map/reduce_scatter | solution.py:322
  150.1 3.0 copy-start.31
  153.1 19.9 %copy-start.7 = (f32[2048,768]{1,0:T(8,128)}, f32[2048,768]{1,0:T(8,128)S(1)}, u32[]{:S(2)}) copy-start(f32[2048,768]{1,0:T(8,128)S(1)} %fusion.60) | copy-start | bytes 18874372
  178.6 79.4 %all-gather.15.cloned.1.call-start = ((), (), s32[]{:S(2)}) async-start(), calls=%async_computation.10 | async-start | bytes 3932160 | tf_op jit(solution)/shard_map/all_gather | solution.py:335
  216.5 5.6 copy-start.6
  219.4 6.8 %copy-start.16 = (f32[512]{0:T(512)}, f32[512]{0:T(512)S(1)}, u32[]{:S(2)}) copy-start(f32[512]{0:T(512)S(1)} %get-tuple-element.136) | copy-start | bytes 6148
  219.4 6.8 %copy-start.17 = (f32[512]{0:T(512)}, f32[512]{0:T(512)S(1)}, u32[]{:S(2)}) copy-start(f32[512]{0:T(512)S(1)} %get-tuple-element.137) | copy-start | bytes 6148
  226.3 93.7 %reduce-scatter.10.cloned.1.call-start = ((), (), s32[]{:S(2)}) async-start(), calls=%async_computation.12 | async-start | bytes 3932160 | tf_op jit(solution)/shard_map/reduce_scatter | solution.py:353
  236.8 7.4 %copy-start.32 = (bf16[2048,768]{0,1:T(8,128)(2,1)S(1)}, bf16[2048,768]{0,1:T(8,128)(2,1)}, u32[]{:S(2)}) copy-start(bf16[2048,768]{0,1:T(8,128)(2,1)} %all-gather.9.cloned.1.call-done) | copy-start | bytes 9437188
  251.8 6.2 %copy-start.10 = (bf16[2048,3,64]{0,2,1:T(8,128)(2,1)S(1)}, bf16[2048,3,64]{0,2,1:T(8,128)(2,1)}, u32[]{:S(2)}) copy-start(bf16[2048,3,64]{0,2,1:T(8,128)(2,1)} %copy.110) | copy-start | bytes 2359300
  263.3 6.5 %copy-start.9 = (bf16[2048,768]{0,1:T(8,128)(2,1)S(1)}, bf16[2048,768]{0,1:T(8,128)(2,1)}, u32[]{:S(2)}) copy-start(bf16[2048,768]{0,1:T(8,128)(2,1)} %all-gather.15.cloned.1.call-done) | copy-start | bytes 9437188
  263.3 6.5 %copy-start.13 = (bf16[192,768]{1,0:T(8,128)(2,1)S(1)}, bf16[192,768]{1,0:T(8,128)(2,1)}, u32[]{:S(2)}) copy-start(bf16[192,768]{1,0:T(8,128)(2,1)} %param.18) | copy-start | bytes 884740
  270.6 146.1 %reduce-scatter.8.cloned.1.call-start = ((), (), s32[]{:S(2)}) async-start(), calls=%async_computation.11 | async-start | bytes 5971968 | tf_op jit(solution)/shard_map/reduce_scatter | solution.py:242
  276.3 201.9 %reduce-scatter.12.cloned.1.call-start = ((), (), s32[]{:S(2)}) async-start(), calls=%async_computation.13 | async-start | bytes 3932160 | tf_op jit(solution)/shard_map/reduce_scatter | solution.py:378
  277.9 42.0 %copy-start.21 = (f32[768]{0:T(1024)S(1)}, f32[768]{0:T(1024)}, u32[]{:S(2)}) copy-start(f32[768]{0:T(1024)} %get-tuple-element.111) | copy-start | bytes 9220
  421.6 13.1 %copy-start.8 = (bf16[2048,3,64]{0,2,1:T(8,128)(2,1)}, bf16[2048,3,64]{0,2,1:T(8,128)(2,1)S(1)}, u32[]{:S(2)}) copy-start(bf16[2048,3,64]{0,2,1:T(8,128)(2,1)S(1)} %copy.117) | copy-start | bytes 2359300
  440.8 130.3 %reduce-scatter.14.cloned.1.call-start = ((), (), s32[]{:S(2)}) async-start(), calls=%async_computation.14 | async-start | bytes 2211840 | tf_op jit(solution)/shard_map/reduce_scatter | solution.py:242
  483.9 3.1 copy-start.20
  (14 other events, 27.9 us)
Sparse Core Ops, SparseCore 0:
  10.2 31.3 all-gather.6
  43.6 28.4 all-gather.8
  73.8 17.4 all-gather.12
  102.5 36.8 all-gather.10
  178.8 37.7 reduce-scatter.5
  226.4 28.4 all-gather.14
  270.7 37.7 reduce-scatter.9
  312.1 104.4 reduce-scatter.7
  440.9 37.3 reduce-scatter.11
  503.5 67.5 reduce-scatter.13
